TPU v7x, 16 devices: a whole 2x2x2 slice. The times are simulated.
16 devices in a mesh: dp: 2 (over z), tp: 8 (over y, x, core).
Axes of the slice: x: 2, y: 2, z: 2, core: 2. Of those that a mesh axis runs over, the one named last changes fastest.
Arguments:
- x: bfloat16 [8192, 3072], P('dp'), parts along dimension 0
- pos: int32 [8192], P('dp'), parts along dimension 0
- g1: bfloat16 [3072], replicated
- g2: bfloat16 [3072], replicated
- wq: bfloat16 [3072, 3072], P(None, 'tp')
- wk: bfloat16 [3072, 1024], replicated
- wv: bfloat16 [3072, 1024], replicated
- wo: bfloat16 [3072, 3072], P('tp')
- wg: bfloat16 [3072, 8192], P(None, 'tp')
- wu: bfloat16 [3072, 8192], P(None, 'tp')
- wd: bfloat16 [8192, 3072], P('tp')
Outputs:
- output 1: bfloat16 [8192, 3072], P('dp'), parts along dimension 0
- output 2: bfloat16 [8192, 8, 128], P('dp', 'tp'), parts along dimension 0
- output 3: bfloat16 [8192, 8, 128], P('dp', 'tp'), parts along dimension 0
There are 2 independent parts. A program takes and returns all parts, laid end to end along the dimension named above; an argument that names none is the same for every part.
All inputs are finite; a program needn't handle non-finite values.
Results may differ from a plain program's by a relative error of at most 0.0160802.
Values are sent between devices in bfloat16 or wider.
A program may use at most 1 GiB of HBM per device.

v0:
```python
import jax
import jax.numpy as jnp
from jax import lax
from jax.sharding import PartitionSpec as P

HEAD = 128
EPS = 1e-5
ROPE_BASE = 500000.0


def _rms(x, g):
    x32 = x.astype(jnp.float32)
    inv = lax.rsqrt(jnp.mean(x32 * x32, axis=-1, keepdims=True) + EPS)
    return (x32 * inv * g.astype(jnp.float32)).astype(jnp.bfloat16)


def _cs(pos, width):
    half = width // 2
    inv = ROPE_BASE ** (-2.0 * jnp.arange(half, dtype=jnp.float32) / width)
    ang = pos.astype(jnp.float32)[..., None] * inv
    return jnp.cos(ang)[..., None, :], jnp.sin(ang)[..., None, :]


def _rope(t, c, s):
    half = t.shape[-1] // 2
    t1, t2 = t[..., :half], t[..., half:]
    return jnp.concatenate([t1 * c - t2 * s, t2 * c + t1 * s], axis=-1)


def _attend(q, k, v, pos_q, pos_k, block, tail):
    tq, tk = q.shape[0], k.shape[0]
    qb = min(tq, block)
    scale = q.shape[-1] ** -0.5
    outs = []
    for i in range(tq // qb):
        lo, hi = i * qb, (i + 1) * qb
        n = tk - tq + hi if tail else tk
        pp = pos_q[lo:hi]
        sc = jnp.einsum("qgrd,kgd->grqk", q[lo:hi], k[:n], preferred_element_type=jnp.float32) * scale
        sc = jnp.where((pos_k[:n][None, :] <= pp[:, None])[None, None], sc, -jnp.inf)
        e = jnp.exp(sc - jnp.max(sc, axis=-1, keepdims=True))
        pr = (e / jnp.sum(e, axis=-1, keepdims=True)).astype(jnp.bfloat16)
        outs.append(jnp.einsum("grqk,kgd->qgrd", pr, v[:n], preferred_element_type=jnp.float32).astype(jnp.bfloat16))
    return jnp.concatenate(outs, axis=0).reshape(tq, -1)


def solution(mesh):
    tp = mesh.shape["tp"]

    def local(x, pos, g1, g2, wq, wk, wv, wo, wg, wu, wd):
        f32, bf = jnp.float32, jnp.bfloat16
        t, d = x.shape
        hl = wq.shape[1] // HEAD
        g = wk.shape[1] // HEAD
        slots = max(g, tp)
        kvl = slots // tp
        r = lax.axis_index("tp")
        start = r * kvl * g // slots
        wk_l = lax.dynamic_slice_in_dim(wk, start * HEAD, kvl * HEAD, axis=1)
        wv_l = lax.dynamic_slice_in_dim(wv, start * HEAD, kvl * HEAD, axis=1)
        a = _rms(x, g1)
        c, s = _cs(pos, HEAD)
        q = _rope(jnp.dot(a, wq, preferred_element_type=f32).reshape(t, hl, HEAD), c, s).astype(bf)
        k = _rope(jnp.dot(a, wk_l, preferred_element_type=f32).reshape(t, kvl, HEAD), c, s).astype(bf)
        v = jnp.dot(a, wv_l, preferred_element_type=f32).astype(bf).reshape(t, kvl, HEAD)
        o = _attend(q.reshape(t, kvl, hl // kvl, HEAD), k, v, pos, pos, 256, True)
        p = jnp.dot(o, wo, preferred_element_type=f32).astype(bf)
        h = (x.astype(f32) + lax.psum(p, "tp").astype(f32)).astype(bf)
        b = _rms(h, g2)
        gt = jnp.dot(b, wg, preferred_element_type=f32)
        up = jnp.dot(b, wu, preferred_element_type=f32)
        u = (jax.nn.silu(gt) * up).astype(bf)
        rr = jnp.dot(u, wd, preferred_element_type=f32).astype(bf)
        y = (h.astype(f32) + lax.psum(rr, "tp").astype(f32)).astype(bf)
        return y, k, v

    return jax.shard_map(
        local,
        mesh=mesh,
        in_specs=(P("dp", None), P("dp"), P(), P(), P(None, "tp"), P(), P(), P("tp", None),
                  P(None, "tp"), P(None, "tp"), P("tp", None)),
        out_specs=(P("dp", None), P("dp", "tp", None), P("dp", "tp", None)),
        check_vma=False,
    )
```

profile of v0, /device:TPU:0, one launch (start us, length us, event | category | flops | bytes accessed | tf_op | source)
XLA Modules:
  0.0 1091.9 jit_solution(11485537974609999288)
XLA Ops:
  11.0 10.3 fusion
  24.2 22.5 %fusion.2 = bf16[4096,3072]{1,0:T(8,128)(2,1)} fusion(bf16[4096,3072]{1,0:T(8,128)(2,1)} %param.11, f32[3072]{0:T(1024)S(1)} %convert_element_type.251, f32[4096]{0:T(1024)S(1)} %add_rsqrt_fusion.1), kind=kLoop, calls=%fused_computation.8 | loop fusion | flops 50331648 | bytes 50360320 | tf_op jit(solution)/shard_map/convert_element_type | solution.py:14
  46.7 12.6 %convolution_convert_fusion.2 = bf16[4096,128]{1,0:T(8,128)(2,1)} fusion(bf16[4096,3072]{1,0:T(8,128)(2,1)} %fusion.2, bf16[3072,1024]{1,0:T(8,128)(2,1)} %param.17, s32[]{:T(128)S(6)} %select_n.74), kind=kOutput, calls=%fused_computation.75 | convolution fusion | flops 3221749760 | bytes 27000836 | tf_op jit(solution)/shard_map/dot_general | solution.py:65
  59.3 14.3 %convolution_bitcast_fusion = f32[4096,1,128]{0,2,1:T(8,128)} fusion(bf16[4096,3072]{1,0:T(8,128)(2,1)} %fusion.2, bf16[3072,1024]{1,0:T(8,128)(2,1)} %param.16, s32[]{:T(128)S(6)} %select_n.74), kind=kOutput, calls=%fused_computation.73 | convolution fusion | flops 3221225472 | bytes 28049412 | tf_op jit(solution)/shard_map/dot_general | solution.py:64
  73.6 18.0 %fusion.407 = f32[4096,384]{0,1:T(8,128)} fusion(bf16[4096,3072]{1,0:T(8,128)(2,1)} %fusion.2, bf16[3072,384]{1,0:T(8,128)(2,1)} %param.15), kind=kOutput, calls=%fused_computation.440 | convolution fusion | flops 9663676416 | bytes 33816576 | tf_op jit(solution)/shard_map/dot_general | solution.py:63
  91.7 9.3 multiply_cosine_fusion
  105.9 6.6 fusion.384
  112.5 5.7 copy.146
  118.2 5.8 copy.145
  124.1 6.8 subtract_convert_fusion
  161.3 5.1 fusion.22
  177.8 5.4 fusion.14
  184.9 6.0 fusion.13
  209.5 5.1 fusion.197
  218.7 5.6 fusion.179
  232.4 6.3 fusion.167
  238.7 5.3 fusion.16
  244.0 6.3 fusion.115
  250.3 5.3 fusion.12
  261.3 6.6 fusion.155
  267.9 6.5 fusion.10
  274.4 7.1 fusion.149
  281.5 6.9 fusion.9
  288.5 7.4 fusion.143
  306.1 19.4 %convolution_convert_fusion.1 = bf16[4096,3072]{1,0:T(8,128)(2,1)} fusion(bf16[4096,384]{0,1:T(8,128)(2,1)} %bitcast.630, bf16[384,3072]{1,0:T(8,128)(2,1)S(1)} %copy-done), kind=kOutput, calls=%fused_computation.15 | convolution fusion | flops 9676259328 | bytes 30670848 | tf_op jit(solution)/shard_map/dot_general | solution.py:67
  326.2 301.2 %all-reduce.3.cloned.1.call-done = bf16[4096,3072]{1,0:T(8,128)(2,1)} async-done(((bf16[4096,3072]{1,0:T(8,128)(2,1)}), bf16[4096,3072]{1,0:T(8,128)(2,1)}) %all-reduce.3.cloned.1.call-update) | async-done | bytes 25165840 | tf_op jit(solution)/shard_map/psum | solution.py:68
  627.4 25.4 %fusion.4 = (f32[4096]{0:T(1024)S(1)}, bf16[4096,3072]{1,0:T(8,128)(2,1)}) fusion(bf16[4096,3072]{1,0:T(8,128)(2,1)} %all-reduce.3.cloned.1.call-done, bf16[4096,3072]{1,0:T(8,128)(2,1)} %param.11), kind=kLoop, calls=%fused_computation.10 | loop fusion | flops 88076288 | bytes 75513856 | tf_op jit(solution)/shard_map/reduce_sum | solution.py:13
  652.8 33.4 %fusion.18 = f32[4096,1024]{1,0:T(8,128)} fusion(bf16[3072,1024]{1,0:T(8,128)(2,1)} %param.19, bf16[4096,3072]{1,0:T(8,128)(2,1)} %get-tuple-element.7, f32[3072]{0:T(1024)S(1)} %convert_element_type.323, f32[4096]{0:T(1024)S(1)} %add_rsqrt_fusion), kind=kOutput, calls=%fused_computation.47 | convolution fusion | flops 25820135424 | bytes 48263168 | tf_op jit(solution)/shard_map/dot_general | solution.py:70
  686.2 35.1 %multiply_convert_fusion = bf16[4096,1024]{1,0:T(8,128)(2,1)} fusion(f32[4096,1024]{1,0:T(8,128)} %fusion.18, bf16[3072,1024]{1,0:T(8,128)(2,1)} %param.20, bf16[4096,3072]{1,0:T(8,128)(2,1)} %get-tuple-element.7, f32[3072]{0:T(1024)S(1)} %convert_element_type.323, f32[4096]{0:T(1024)S(1)} %add_rsqrt_fusion), kind=kOutput, calls=%fused_computation.16 | convolution fusion | flops 25845301248 | bytes 56651776 | tf_op jit(solution)/shard_map/dot_general | solution.py:71
  721.3 34.4 %convolution_convert_fusion = bf16[4096,3072]{1,0:T(8,128)(2,1)} fusion(bf16[4096,1024]{1,0:T(8,128)(2,1)} %multiply_convert_fusion, bf16[1024,3072]{1,0:T(8,128)(2,1)} %param.21), kind=kOutput, calls=%fused_computation.14 | convolution fusion | flops 25782386688 | bytes 39845888 | tf_op jit(solution)/shard_map/dot_general | solution.py:73
  758.3 296.6 %all-reduce.5.cloned.1.call-done = bf16[4096,3072]{1,0:T(8,128)(2,1)} async-done(((bf16[4096,3072]{1,0:T(8,128)(2,1)}), bf16[4096,3072]{1,0:T(8,128)(2,1)}) %all-reduce.5.cloned.1.call-update) | async-done | bytes 25165840 | tf_op jit(solution)/shard_map/psum | solution.py:74
  1054.9 30.0 %fusion.7 = bf16[4096,3072]{1,0:T(8,128)(2,1)} fusion(bf16[4096,3072]{1,0:T(8,128)(2,1)} %get-tuple-element.7, bf16[4096,3072]{1,0:T(8,128)(2,1)} %all-reduce.5.cloned.1.call-done), kind=kLoop, calls=%fused_computation.13 | loop fusion | flops 50331648 | bytes 75497472 | tf_op jit(solution)/shard_map/convert_element_type | solution.py:74
  (142 shorter events, 104.7 us)
Async XLA Ops:
  7.2 298.9 %copy-start = (bf16[384,3072]{1,0:T(8,128)(2,1)S(1)}, bf16[384,3072]{1,0:T(8,128)(2,1)}, u32[]{:S(2)}) copy-start(bf16[384,3072]{1,0:T(8,128)(2,1)} %param.18) | copy-start | bytes 7077892
  7.2 620.2 %all-reduce.3.cloned.1.call-start = ((), (), s32[]{:S(2)}) async-start(), calls=%async_computation | async-start | bytes 50331648 | tf_op jit(solution)/shard_map/psum | solution.py:68
  7.2 84.4 %copy-start.22 = (f32[64]{0:T(128)}, f32[64]{0:T(128)S(1)}, u32[]{:S(2)}) copy-start(f32[64]{0:T(128)S(1)} %multiply_power_fusion) | copy-start | bytes 772
  11.0 10.5 copy-start.14
  91.7 9.3 copy-start.9
  105.8 190.1 %copy-start.2 = (bf16[4096,1,64]{0,2,1:T(8,128)(2,1)}, bf16[4096,1,64]{0,2,1:T(8,128)(2,1)S(1)}, u32[]{:S(2)}) copy-start(bf16[4096,1,64]{0,2,1:T(8,128)(2,1)S(1)} %get-tuple-element.12) | copy-start | bytes 1572868
  105.9 190.1 %copy-start.4 = (bf16[4096,1,64]{0,2,1:T(8,128)(2,1)}, bf16[4096,1,64]{0,2,1:T(8,128)(2,1)S(1)}, u32[]{:S(2)}) copy-start(bf16[4096,1,64]{0,2,1:T(8,128)(2,1)S(1)} %get-tuple-element.13) | copy-start | bytes 1572868
  118.2 5.8 slice-start.2
  118.2 5.8 copy-start.20
  133.1 2.0 slice-start.3
  133.2 2.0 copy-start.18
  135.4 2.4 copy-start.12
  135.4 2.4 slice-start.8
  135.4 2.4 copy-start.17
  139.3 3.2 slice-start.6
  142.8 3.6 copy-start.10
  142.8 3.6 slice-start.5
  146.9 4.0 slice-start.11
  155.1 4.8 slice-start.9
  161.3 5.1 copy-start.15
  174.2 2.0 copy-start.21
  190.9 3.9 copy-start.23
  192.5 3.4 copy-start.8
  196.5 2.0 copy-start.7
  196.5 2.0 copy-start.13
  201.0 2.2 slice-start
  201.5 1.9 slice-start.1
  205.6 3.9 copy-start.24
  255.6 2.1 copy-start.25
  288.4 7.5 copy-start.6
  325.5 729.4 %all-reduce.5.cloned.1.call-start = ((), (), s32[]{:S(2)}) async-start(), calls=%async_computation.1 | async-start | bytes 50331648 | tf_op jit(solution)/shard_map/psum | solution.py:74
  1054.9 30.0 %copy-start.1 = (bf16[384,3072]{1,0:T(8,128)(2,1)S(1)}, bf16[384,3072]{1,0:T(8,128)(2,1)}, u32[]{:S(2)}) copy-start(bf16[384,3072]{1,0:T(8,128)(2,1)} %param.18) | copy-start | bytes 7077892
  (8 other events, 8.3 us)
Sparse Core Ops, SparseCore 0:
  325.7 301.7 all-reduce.2
  755.9 298.9 all-reduce.4
where the time goes:
time: 1100 us; the launch traced here: 1090 us
  waiting for transfers between devices  598 us (54%)
  matrix products  282 us (26%)
  other arithmetic  172 us (16%)
  local copies, waits for them, and re-layouts  24.6 us (2%)
  between operations  14.7 us (1%)
    psum x1, waiting for transfers between devices, local(): h = (x.astype(f32) + lax.psum(p, 'tp').astype(f32)).astype(bf)  301 us
    psum x1, waiting for transfers between devices, local(): y = (h.astype(f32) + lax.psum(rr, 'tp').astype(f32)).astype(bf)  297 us
    dot_general x16, matrix products, _attend(): jnp.einsum('grqk,kgd->qgrd', pr, v[:n], preferred_element_type=jnp.float32)  64.8 us
    dot_general x16, matrix products, _attend(): jnp.einsum('qgrd,kgd->grqk', q[lo:hi], k[:n], preferred_element_type=jnp....  50.3 us
    reduce_sum x16, other arithmetic, _attend(): pr = (e / jnp.sum(e, axis=-1, keepdims=True)).astype(jnp.bfloat16)  46.9 us
    reduce_sum x2, other arithmetic, _rms(): inv = lax.rsqrt(jnp.mean(x32 * x32, axis=-1, keepdims=True) + EPS)  35.7 us
    dot_general x1, matrix products, local(): up = jnp.dot(b, wu, preferred_element_type=f32)  35.1 us
    dot_general x1, matrix products, local(): rr = jnp.dot(u, wd, preferred_element_type=f32).astype(bf)  34.4 us
  transfers between devices with their start and end apart: 2, of which 2 were waited for; matrix products, arithmetic and copies ran while one was open for 0% of the time, Pallas kernels for 0%

commit v1 on v0

v1 whole, which is shorter than its diff:
```python
import functools

import jax
import jax.numpy as jnp
from jax import lax
from jax.experimental import pallas as pl
from jax.experimental.pallas import tpu as pltpu
from jax.sharding import PartitionSpec as P

HEAD = 128
EPS = 1e-5
ROPE_BASE = 500000.0
LOG2E = 1.4426950408889634
NCHUNK = 4
MESH = pl.DeviceIdType.MESH
F32, BF = jnp.float32, jnp.bfloat16
ANY = pl.BlockSpec(memory_space=pl.ANY)


def _pos_of(r):
    return (r % 2) * 4 + r // 2


def _qkv_kernel(nb, x_ref, g_ref, c_ref, s_ref, wq_ref, wk_ref, wv_ref, q_ref, k_ref, v_ref, w, a, sems):
    i = pl.program_id(0)
    r = lax.axis_index("tp")
    tm = x_ref.shape[0]
    nq = wq_ref.shape[1]

    @pl.when(i == 0)
    def _():
        col = pl.ds(pl.multiple_of(r * HEAD, HEAD), HEAD)
        cps = [
            pltpu.make_async_copy(wq_ref, w.at[:, pl.ds(0, nq)], sems.at[0]),
            pltpu.make_async_copy(wk_ref.at[:, col], w.at[:, pl.ds(nq, HEAD)], sems.at[1]),
            pltpu.make_async_copy(wv_ref.at[:, col], w.at[:, pl.ds(nq + HEAD, HEAD)], sems.at[2]),
        ]
        for cp in cps:
            cp.start()
        for cp in cps:
            cp.wait()

    _norm_rows(x_ref, g_ref, a, tm)
    first = i < nb // 2
    lane = lax.broadcasted_iota(jnp.int32, (tm, HEAD), 1)
    low = lane < HEAD // 2
    keep = jnp.logical_xor(low, jnp.logical_not(first))
    cb, sb = c_ref[...], s_ref[...]
    c = jnp.where(keep, cb, pltpu.roll(cb, HEAD // 2, 1))
    s = jnp.where(keep, sb, pltpu.roll(sb, HEAD // 2, 1))
    s = jnp.where(low, -s, s)
    z = jnp.dot(a[...], w[...], preferred_element_type=F32)
    for h in range(nq // HEAD + 1):
        t = z[:, h * HEAD:(h + 1) * HEAD]
        t = (t * c + pltpu.roll(t, HEAD // 2, 1) * s).astype(BF)
        if h < nq // HEAD:
            q_ref[:, h * HEAD:(h + 1) * HEAD] = t
        else:
            k_ref[...] = t
    v_ref[...] = z[:, nq + HEAD:].astype(BF)


def _norm_rows(src, g_ref, dst, rows, step=16):
    @pl.loop(0, rows // step, unroll=2)
    def _(n):
        sl = pl.ds(pl.multiple_of(n * step, step), step)
        t = src[sl, :].astype(F32)
        inv = lax.rsqrt(jnp.mean(t * t, axis=-1, keepdims=True) + EPS)
        dst[sl, :] = (t * inv * g_ref[...].astype(F32)).astype(BF)


def _big_kernel(J, R, QB, x_ref, q_ref, k_ref, v_ref, wo_ref, g2_ref, wg_ref, wu_ref, wd_ref,
                y_ref, oland, bland, rs1land,
                wg, wu, wd, rs2x, rs2y, rs3a, rs3b, hk, own,
                a2s, a2r, abs_, abr, ays, ayr, rss, rsr, lsem, wsem):
    me = lax.axis_index("tp")
    c, s = me // 2, me % 2
    D = x_ref.shape[1]
    H = D // 2
    T = x_ref.shape[0]
    C = 8 * R
    R4 = 4 * R
    hq = q_ref.shape[1]
    cx = c + 1 - 2 * (c % 2)
    cy = (c + 2) % 4
    cd = 3 - c
    dev = lambda chip, core: chip * 2 + core
    X, Y, PT = dev(cx, s), dev(cy, s), dev(c, 1 - s)
    mypos = s * 4 + c
    px, py, pd = s * 4 + cx, s * 4 + cy, s * 4 + cd

    def rcopy(src, dst, ss, rs, to):
        return pltpu.make_async_remote_copy(src_ref=src, dst_ref=dst, send_sem=ss, recv_sem=rs,
                                            device_id={"tp": to}, device_id_type=MESH)

    wcp = [pltpu.make_async_copy(wg_ref, wg, wsem.at[0]), pltpu.make_async_copy(wu_ref, wu, wsem.at[1]),
           pltpu.make_async_copy(wd_ref, wd, wsem.at[2])]

    bar = pltpu.get_barrier_semaphore()
    for m in range(1, 8):
        pl.semaphore_signal(bar, inc=1, device_id={"tp": (me + m) % 8}, device_id_type=MESH)
    pl.semaphore_wait(bar, 7)

    def peer(m):
        return (me + m) % 8

    def frm(m):
        return (me + 8 - m) % 8

    def a2a(j, m, o):
        to = peer(m)
        return rcopy(o.at[pl.ds(pl.multiple_of(j * C + _pos_of(to) * R, R), R), :],
                     oland.at[pl.ds(pl.multiple_of(j * R, R), R), pl.ds(pl.multiple_of(me * hq, HEAD), hq)],
                     a2s.at[j, m], a2r.at[j, m], to)

    def a2a_land(j, m):
        return oland.at[pl.ds(pl.multiple_of(j * R, R), R), pl.ds(pl.multiple_of(frm(m) * hq, HEAD), hq)]

    def attention(q, k, v, o, acc, mm, ll, asem):
        cps = [pltpu.make_async_copy(q_ref, q, asem.at[0]), pltpu.make_async_copy(k_ref, k, asem.at[1]),
               pltpu.make_async_copy(v_ref, v, asem.at[2])]
        for cp in cps:
            cp.start()
        for cp in wcp:
            cp.start()
        for cp in cps:
            cp.wait()
        nh = hq // HEAD
        sc = (HEAD ** -0.5) * LOG2E

        def block(row, kb, masked):
            kv = pl.ds(pl.multiple_of(kb * QB, QB), QB)
            kk, vv = k[kv, :], v[kv, :]
            for h in range(nh):
                qq = q[row, h * HEAD:(h + 1) * HEAD]
                sco = lax.dot_general(qq, kk, (((1,), (1,)), ((), ())), preferred_element_type=F32) * sc
                if masked:
                    ri = lax.broadcasted_iota(jnp.int32, (QB, QB), 0)
                    ci = lax.broadcasted_iota(jnp.int32, (QB, QB), 1)
                    sco = jnp.where(ci <= ri, sco, -jnp.inf)
                mo = mm[h, :, :1]
                mn = jnp.maximum(mo, jnp.max(sco, axis=-1, keepdims=True))
                al = jnp.exp2(mo - mn)
                p = jnp.exp2(sco - mn)
                ll[h] = ll[h] * al + jnp.sum(p, axis=-1, keepdims=True)
                acc[h] = acc[h] * al + jnp.dot(p.astype(BF), vv, preferred_element_type=F32)
                mm[h] = jnp.broadcast_to(mn, (QB, HEAD))

        @pl.loop(0, T // QB)
        def _(i):
            row = pl.ds(pl.multiple_of(i * QB, QB), QB)
            acc[...] = jnp.zeros_like(acc)
            ll[...] = jnp.zeros_like(ll)
            mm[...] = jnp.full_like(mm, -jnp.inf)

            @pl.loop(0, i)
            def _(kb):
                block(row, kb, False)

            block(row, i, True)
            for h in range(nh):
                o[row, h * HEAD:(h + 1) * HEAD] = (acc[h] / ll[h]).astype(BF)

            per = C // QB

            @pl.when(i % per == per - 1)
            def _():
                j = i // per
                for m in range(1, 8):
                    a2a(j, m, o).start()
                pltpu.make_async_copy(
                    o.at[pl.ds(pl.multiple_of(j * C + mypos * R, R), R), :],
                    oland.at[pl.ds(pl.multiple_of(j * R, R), R), pl.ds(pl.multiple_of(me * hq, HEAD), hq)],
                    a2s.at[j, 0]).start()

        @pl.loop(0, J)
        def _(j):
            pltpu.make_async_copy(
                o.at[pl.ds(pl.multiple_of(j * C + mypos * R, R), R), :],
                oland.at[pl.ds(pl.multiple_of(j * R, R), R), pl.ds(pl.multiple_of(me * hq, HEAD), hq)],
                a2s.at[j, 0]).wait()
            for m in range(1, 8):
                a2a(j, m, o).wait_send()

    pl.run_scoped(attention, pltpu.VMEM((T, hq), BF), pltpu.VMEM((T, HEAD), BF), pltpu.VMEM((T, HEAD), BF),
                  pltpu.VMEM((T, hq), BF), pltpu.VMEM((hq // HEAD, QB, HEAD), F32),
                  pltpu.VMEM((hq // HEAD, QB, HEAD), F32), pltpu.VMEM((hq // HEAD, QB, HEAD), F32),
                  pltpu.SemaphoreType.DMA((3,)))

    NT = min(512, D)

    def oproj(oo, wt, osem, tsem):
        for j in range(J):
            pltpu.make_async_copy(x_ref.at[pl.ds(pl.multiple_of(j * C + mypos * R, R), R), :],
                                  hk.at[pl.ds(j * R, R), :], osem.at[1 + j]).start()

        def tile(n, slot):
            return pltpu.make_async_copy(wo_ref.at[:, pl.ds(pl.multiple_of(n * NT, NT), NT)], wt.at[slot],
                                         tsem.at[slot])

        tile(0, 0).start()

        @pl.loop(0, J)
        def _(j):
            for m in range(1, 8):
                pltpu.make_async_remote_copy(src_ref=a2a_land(j, m), dst_ref=a2a_land(j, m), send_sem=a2s.at[j, m],
                                             recv_sem=a2r.at[j, m], device_id={"tp": frm(m)},
                                             device_id_type=MESH).wait_recv()

        cp = pltpu.make_async_copy(oland, oo, osem.at[0])
        cp.start()
        cp.wait()
        for j in range(J):
            pltpu.make_async_copy(x_ref.at[pl.ds(pl.multiple_of(j * C + mypos * R, R), R), :],
                                  hk.at[pl.ds(j * R, R), :], osem.at[1 + j]).wait()
        nt = D // NT

        @pl.loop(0, nt)
        def _(n):
            slot = n % 2

            @pl.when(n + 1 < nt)
            def _():
                tile(n + 1, 1 - slot).start()

            tile(n, slot).wait()
            col = pl.ds(pl.multiple_of(n * NT, NT), NT)
            hk[:, col] = (hk[:, col].astype(F32)
                          + jnp.dot(oo[...], wt[slot], preferred_element_type=F32)).astype(BF)

        _norm_rows(hk, g2_ref, own, J * R)

    pl.run_scoped(oproj, pltpu.VMEM((J * R, 8 * hq), BF), pltpu.VMEM((2, 8 * hq, NT), BF), pltpu.SemaphoreType.DMA((1 + J,)),
                  pltpu.SemaphoreType.DMA((2,)))

    R2 = R // 2

    def rows(land, j, pos, off=0, n=R):
        return land.at[pl.ds(pl.multiple_of(j * C + pos * R + off, R2), n), :]

    def ownrows(j):
        return own.at[pl.ds(pl.multiple_of(j * R, R), R), :]

    def g_copy(land, ss, rs, j, i):
        k = dict(ss=ss.at[j, i], rs=rs.at[j, i])
        if i < 3:
            return rcopy(ownrows(j), rows(land, j, mypos), to=(X, Y, PT)[i], **k)
        if i == 3:
            return rcopy(rows(land, j, px, 0, R2), rows(land, j, px, 0, R2), to=Y, **k)
        if i == 4:
            return rcopy(rows(land, j, py, R2, R2), rows(land, j, py, R2, R2), to=X, **k)
        if i == 5:
            return rcopy(rows(land, j, px), rows(land, j, px), to=PT, **k)
        if i == 6:
            return rcopy(rows(land, j, py), rows(land, j, py), to=PT, **k)
        off = 0 if i == 7 else R2
        return rcopy(rows(land, j, pd, off, R2), rows(land, j, pd, off, R2), to=PT, **k)

    def g_recv(land, ss, rs, j, i):
        o4 = (1 - s) * 4
        src = [(px, 0, R), (py, 0, R), (o4 + c, 0, R), (pd, 0, R2), (pd, R2, R2), (o4 + cx, 0, R), (o4 + cy, 0, R),
               (o4 + cd, 0, R2), (o4 + cd, R2, R2)][i]
        d = rows(land, j, *src)
        rcopy(d, d, ss.at[j, i], rs.at[j, i], PT).wait_recv()

    def g_local(land, j, kind):
        return pltpu.make_async_copy(ownrows(j), rows(land, j, mypos), lsem.at[kind, j])

    def g_own(land, ss, rs, j, kind):
        for i in range(3):
            g_copy(land, ss, rs, j, i).start()
        g_local(land, j, kind).start()

    def g_fwd(land, ss, rs, j):
        g_recv(land, ss, rs, j, 0)
        g_copy(land, ss, rs, j, 3).start()
        g_recv(land, ss, rs, j, 1)
        g_copy(land, ss, rs, j, 4).start()
        g_copy(land, ss, rs, j, 5).start()
        g_copy(land, ss, rs, j, 6).start()

    def g_fwd2(land, ss, rs, j):
        for i in (3, 4):
            g_recv(land, ss, rs, j, i)
            g_copy(land, ss, rs, j, i + 4).start()

    def g_finish(land, ss, rs, j):
        for i in (2, 5, 6, 7, 8):
            g_recv(land, ss, rs, j, i)

    gb = (bland, abs_, abr)
    gy = (y_ref, ays, ayr)

    def ew(n, f):
        @pl.loop(0, n // 16)
        def _(i):
            f(pl.ds(pl.multiple_of(i * 16, 16), 16))

    def mlp(bt, us, pb, rt, sums, bsem):
        def sumsl(j, chip, col):
            return sums.at[j % 2, pl.ds(pl.multiple_of(chip * R, R), R), col]

        lo, hi = pl.ds(0, H), pl.ds(H, H)

        def rs_copy(j, i):
            k = dict(ss=rss.at[j, i], rs=rsr.at[j, i])
            if i == 0:
                return rcopy(pb.at[0], rs1land.at[j], to=PT, **k)
            if i == 1:
                return rcopy(sumsl(j, cx, lo), rs2x.at[j, 0], to=X, **k)
            if i == 2:
                return rcopy(sumsl(j, cd, lo), rs2x.at[j, 1], to=X, **k)
            if i == 3:
                return rcopy(sumsl(j, cy, hi), rs2y.at[j, 0], to=Y, **k)
            if i == 4:
                return rcopy(sumsl(j, cd, hi), rs2y.at[j, 1], to=Y, **k)
            if i == 5:
                return rcopy(sumsl(j, cy, lo), rs3a.at[j], to=Y, **k)
            return rcopy(sumsl(j, cx, hi), rs3b.at[j], to=X, **k)

        def load_b(j, half):
            pos = jnp.where(half == 0, 1 - s, s) * 4 if not isinstance(half, int) else ((1 - s) if half == 0 else s) * 4
            return pltpu.make_async_copy(bland.at[pl.ds(pl.multiple_of(j * C + pos * R, R4), R4), :], bt.at[half],
                                         bsem.at[half])

        def compute(j):
            for half in range(2):
                load_b(j, half).start()
            for half in range(2):
                load_b(j, half).wait()
                if half == 0:
                    @pl.when(j >= 1)
                    def _():
                        rs_copy(j - 1, 0).wait_send()

                @pl.loop(0, us.shape[1] // 256)
                def _(n):
                    col = pl.ds(pl.multiple_of(n * 256, 256), 256)
                    g = jnp.dot(bt[half], wg[:, col], preferred_element_type=F32)
                    u = jnp.dot(bt[half], wu[:, col], preferred_element_type=F32)
                    us[:, col] = (g * jax.nn.sigmoid(g) * u).astype(BF)

                @pl.loop(0, D // 512)
                def _(n):
                    col = pl.ds(pl.multiple_of(n * 512, 512), 512)
                    pb[half, :, col] = jnp.dot(us[...], wd[:, col], preferred_element_type=F32).astype(BF)

                if half == 0:
                    rs_copy(j, 0).start()

            rs_copy(j, 0).wait_recv()
            cp = pltpu.make_async_copy(rs1land.at[j], rt, bsem.at[0])
            cp.start()
            cp.wait()

            @pl.when(j >= 2)
            def _():
                for i in range(1, 7):
                    rs_copy(j - 2, i).wait_send()

            def add(sl):
                sums[j % 2, sl, :] = (pb[1, sl, :].astype(F32) + rt[sl, :].astype(F32)).astype(BF)

            ew(R4, add)
            for i in (1, 3, 2, 4):
                rs_copy(j, i).start()

        def rs3(j):
            for i in (1, 3, 2, 4):
                rs_copy(j, i).wait_recv()

            def addy(sl):
                b = pl.ds(pl.multiple_of(cy * R + sl.start, 16), 16)
                sums[j % 2, b, lo] = (sums[j % 2, b, lo].astype(F32) + rs2x[j, 1, sl, :].astype(F32)).astype(BF)
                b = pl.ds(pl.multiple_of(cx * R + sl.start, 16), 16)
                sums[j % 2, b, hi] = (sums[j % 2, b, hi].astype(F32) + rs2y[j, 1, sl, :].astype(F32)).astype(BF)

            ew(R, addy)
            rs_copy(j, 5).start()
            rs_copy(j, 6).start()

        def final(j):
            rs_copy(j, 5).wait_recv()
            rs_copy(j, 6).wait_recv()
            for i in range(3):
                g_copy(*gb, j, i).wait_send()

            def fin(sl):
                b = pl.ds(pl.multiple_of(c * R + sl.start, 16), 16)
                o = pl.ds(pl.multiple_of(j * R + sl.start, 16), 16)
                for col, r2, r3 in ((lo, rs2x, rs3a), (hi, rs2y, rs3b)):
                    t = (sums[j % 2, b, col].astype(F32) + r2[j, 0, sl, :].astype(F32)) + r3[j, sl, :].astype(F32)
                    own[o, col] = (hk[o, col].astype(F32) + t).astype(BF)

            ew(R, fin)
            g_own(*gy, j, 1)

        g_own(*gb, 0, 0)
        for cp in wcp:
            cp.wait()

        @pl.loop(0, J + 2)
        def _(t):
            @pl.when(t < J)
            def _():
                g_fwd(*gb, t)

            @pl.when(jnp.logical_and(t >= 1, t <= J))
            def _():
                rs3(t - 1)

            @pl.when(t >= 2)
            def _():
                g_fwd(*gy, t - 2)

            @pl.when(t + 1 < J)
            def _():
                g_own(*gb, t + 1, 0)

            @pl.when(t < J)
            def _():
                g_fwd2(*gb, t)

            @pl.when(jnp.logical_and(t >= 1, t <= J))
            def _():
                final(t - 1)

            @pl.when(t < J)
            def _():
                g_finish(*gb, t)
                g_local(bland, t, 0).wait()
                compute(t)

            @pl.when(t >= 2)
            def _():
                g_fwd2(*gy, t - 2)

        rs_copy(J - 1, 0).wait_send()
        for j in range(max(J - 2, 0), J):
            for i in range(1, 7):
                rs_copy(j, i).wait_send()

    pl.run_scoped(mlp, pltpu.VMEM((2, R4, D), BF), pltpu.VMEM((R4, wg.shape[1]), BF), pltpu.VMEM((2, R4, D), BF),
                  pltpu.VMEM((R4, D), BF), pltpu.VMEM((2, R4, D), BF), pltpu.SemaphoreType.DMA((2,)))

    @pl.loop(0, J)
    def _(j):
        g_finish(*gy, j)
        for i in range(3, 9):
            g_copy(*gb, j, i).wait_send()
        for i in range(9):
            g_copy(*gy, j, i).wait_send()
        g_local(y_ref, j, 1).wait()


def _tables(pos):
    half = HEAD // 2
    inv = ROPE_BASE ** (-2.0 * jnp.arange(half, dtype=F32) / HEAD)
    t = pos.shape[0]
    p = pos.astype(F32)
    lane = lax.broadcasted_iota(jnp.int32, (t // 2, HEAD), 1)
    pp = jnp.where(lane < half, p[:t // 2, None], p[t // 2:, None])
    ang = pp * jnp.concatenate([inv, inv])[None, :]
    return jnp.cos(ang), jnp.sin(ang)


def solution(mesh):
    def local(x, pos, g1, g2, wq, wk, wv, wo, wg, wu, wd):
        t, d = x.shape
        hq = wq.shape[1]
        ff = wg.shape[1]
        wo_full = lax.all_gather(wo, "tp", axis=0, tiled=True)
        cs, sn = _tables(pos)
        tm = min(512, t // 2)
        nb = t // tm
        row = lambda i: (i, 0)
        q, k, v = pl.pallas_call(
            functools.partial(_qkv_kernel, nb),
            grid=(nb,),
            in_specs=[pl.BlockSpec((tm, d), row), pl.BlockSpec((1, d), lambda i: (0, 0)),
                      pl.BlockSpec((tm, HEAD), lambda i: (i % (nb // 2), 0)),
                      pl.BlockSpec((tm, HEAD), lambda i: (i % (nb // 2), 0)), ANY, ANY, ANY],
            out_specs=[pl.BlockSpec((tm, hq), row), pl.BlockSpec((tm, HEAD), row), pl.BlockSpec((tm, HEAD), row)],
            out_shape=[jax.ShapeDtypeStruct((t, hq), BF), jax.ShapeDtypeStruct((t, HEAD), BF),
                       jax.ShapeDtypeStruct((t, HEAD), BF)],
            scratch_shapes=[pltpu.VMEM((d, hq + 2 * HEAD), BF), pltpu.VMEM((tm, d), BF),
                            pltpu.SemaphoreType.DMA((3,))],
            compiler_params=pltpu.CompilerParams(dimension_semantics=("arbitrary",), vmem_limit_bytes=40 << 20),
            cost_estimate=pl.CostEstimate(flops=2 * t * d * (hq + 2 * HEAD), bytes_accessed=2 * t * d,
                                          transcendentals=0),
            name="qkv",
        )(x, g1.reshape(1, d), cs, sn, wq, wk, wv)

        J = NCHUNK
        R = t // 8 // J
        QB = min(512, 8 * R)
        dma = pltpu.SemaphoreType.DMA
        y, _, _, _ = pl.pallas_call(
            functools.partial(_big_kernel, J, R, QB),
            in_specs=[ANY] * 5 + [pl.BlockSpec(memory_space=pltpu.VMEM)] + [ANY] * 3,
            out_specs=[ANY] * 4,
            out_shape=[jax.ShapeDtypeStruct((t, d), BF), jax.ShapeDtypeStruct((J * R, 8 * hq), BF),
                       jax.ShapeDtypeStruct((t, d), BF), jax.ShapeDtypeStruct((J, 4 * R, d), BF)],
            scratch_shapes=[pltpu.VMEM((d, ff), BF), pltpu.VMEM((d, ff), BF), pltpu.VMEM((ff, d), BF),
                            pltpu.VMEM((J, 2, R, d // 2), BF), pltpu.VMEM((J, 2, R, d // 2), BF),
                            pltpu.VMEM((J, R, d // 2), BF), pltpu.VMEM((J, R, d // 2), BF),
                            pltpu.VMEM((J * R, d), BF), pltpu.VMEM((J * R, d), BF),
                            dma((J, 8)), dma((J, 8)), dma((J, 9)), dma((J, 9)), dma((J, 9)), dma((J, 9)),
                            dma((J, 7)), dma((J, 7)), dma((2, J)), dma((3,))],
            compiler_params=pltpu.CompilerParams(collective_id=0, has_side_effects=True,
                                                 vmem_limit_bytes=67043328),
            cost_estimate=pl.CostEstimate(flops=2 * t * d * ff * 3, bytes_accessed=2 * t * d * 6, transcendentals=0),
            name="layer",
        )(x, q, k, v, wo_full, g2.reshape(1, d), wg, wu, wd)
        return y, k.reshape(t, 1, HEAD), v.reshape(t, 1, HEAD)

    return jax.shard_map(
        local,
        mesh=mesh,
        in_specs=(P("dp", None), P("dp"), P(), P(), P(None, "tp"), P(), P(), P("tp", None),
                  P(None, "tp"), P(None, "tp"), P("tp", None)),
        out_specs=(P("dp", None), P("dp", "tp", None), P("dp", "tp", None)),
        check_vma=False,
    )
```

time: 1100 us -> 634 us (0.58)
  waiting for transfers between devices: 598 us -> 41.8 us
  Pallas kernels: 0 us -> 544 us
  matrix products: 282 us -> 0 us
  other arithmetic: 172 us -> 4.56 us
    psum x2 -> x0, waiting for transfers between devices: 598 us -> none  [the longest x1 301 us: local(): h = (x.astype(f32) + lax.psum(p, 'tp').astype(f32)).astype(bf)]
    pallas_call x0 -> x2, Pallas kernels: none -> 544 us  [the longest x1 498 us: local(): pl.pallas_call(functools.partial(_big_kernel, J, R, QB), in_specs=[ANY] *...]
    dot_general x39 -> x0, matrix products: 282 us -> none  [the longest x16 64.8 us: _attend(): jnp.einsum('grqk,kgd->qgrd', pr, v[:n], preferred_element_type=jnp.float32)]
    reduce_sum x18 -> x0, other arithmetic: 82.6 us -> none  [the longest x16 46.9 us: _attend(): pr = (e / jnp.sum(e, axis=-1, keepdims=True)).astype(jnp.bfloat16)]
    convert_element_type x5 -> x1, other arithmetic: 53.9 us -> 0.72 us  [_tables(): p = pos.astype(F32)]
    all_gather x0 -> x1, waiting for transfers between devices: none -> 41.1 us  [local(): wo_full = lax.all_gather(wo, 'tp', axis=0, tiled=True)]
    le x16 -> x0, other arithmetic: 14.7 us -> none  [_attend(): pos_k[:n][None, :] <= pp[:, None]]
    another operation x2 -> x0, other arithmetic: 11.7 us -> none
  transfers between devices with their start and end apart: 2 -> 1, of which waited for: 2 -> 1; matrix products, arithmetic and copies ran while one was open for 0% -> 1% of each run, Pallas kernels for 0% -> 7%
where the time goes in v1:
time: 634 us; the launch traced here: 633 us
  Pallas kernels  544 us (86%)
  waiting for transfers between devices  41.8 us (7%)
  local copies, waits for them, and re-layouts  28.8 us (5%)
  between operations  14.1 us (2%)
    pallas_call x1, Pallas kernels, local(): pl.pallas_call(functools.partial(_big_kernel, J, R, QB), in_specs=[ANY] *...  498 us
    pallas_call x1, Pallas kernels, local(): pl.pallas_call(functools.partial(_qkv_kernel, nb), grid=(nb,), in_specs=[...  45.8 us
    all_gather x1, waiting for transfers between devices, local(): wo_full = lax.all_gather(wo, 'tp', axis=0, tiled=True)  41.1 us
    unnamed x7, local copies, waits for them, and re-layouts  26.8 us
  transfers between devices with their start and end apart: 1, of which 1 were waited for; matrix products, arithmetic and copies ran while one was open for 1% of the time, Pallas kernels for 7%

profile of v1, /device:TPU:0, one launch (start us, length us, event | category | flops | bytes accessed | tf_op | source)
XLA Modules:
  0.0 633.4 jit_solution(8717076151379416989)
XLA Ops:
  7.2 0.0 all-gather.2.cloned.1.call-start
  7.2 0.7 all-gather.2.cloned.1.call-update
  7.9 0.7 reshape.21.g_ref
  8.6 1.3 reshape.22.g2_ref
  9.9 0.7 convert_element_type.3
  10.6 0.1 pad_maximum_fusion
  10.7 3.7 fusion
  14.5 0.0 copy-start
  14.5 2.8 copy-done
  17.2 0.0 copy-start.1
  17.2 1.7 copy-done.1
  18.9 45.8 %qkv.1 = (bf16[4096,384]{1,0:T(8,128)(2,1)S(1)}, bf16[4096,128]{1,0:T(8,128)(2,1)}, bf16[4096,128]{1,0:T(8,128)(2,1)}) custom-call(bf16[4096,3072]{1,0:T(8,128)(2,1)} %x_ref.3, bf16[1,3072]{1,0:T(2,128)(2,1)S(1)} %reshape.21.g_ref, f32[2048,128]{1,0:T(8,128)S(1)} %get-tuple-element.12.c_ref, f32[2048,128]{1,0:T(8,128)S(1)} %get-tuple-element.11.s_ref, ...), custom_call_target="tpu_custom_call" | custom-call | flops 16106127360 | bytes 25165824 | tf_op jit(solution)/shard_map/qkv/pallas_call | solution.py:477
  64.7 0.0 copy-start.2
  64.7 1.7 copy-done.2
  66.4 41.1 %all-gather.2.cloned.1.call-done.wo_ref = bf16[3072,3072]{1,0:T(8,128)(2,1)} async-done(((bf16[384,3072]{1,0:T(8,128)(2,1)}), bf16[3072,3072]{1,0:T(8,128)(2,1)}) %all-gather.2.cloned.1.call-update) | async-done | bytes 18874384 | tf_op jit(solution)/shard_map/all_gather | solution.py:472
  107.5 498.4 %layer.1 = (bf16[4096,3072]{1,0:T(8,128)(2,1)}, bf16[512,3072]{1,0:T(8,128)(2,1)}, bf16[4096,3072]{1,0:T(8,128)(2,1)}, bf16[4,512,3072]{2,1,0:T(8,128)(2,1)}) custom-call(bf16[4096,3072]{1,0:T(8,128)(2,1)} %x_ref.3, bf16[4096,384]{1,0:T(8,128)(2,1)} %copy-done.2, bf16[4096,128]{1,0:T(8,128)(2,1)} %get-tuple-element.8.k_ref, ...), custom_call_target="tpu_custom_call" | custom-call | flops 77309411328 | bytes 150994944 | tf_op jit(solution)/shard_map/layer/pallas_call | solution.py:498
  605.9 20.7 %copy.15 = bf16[4096,3072]{1,0:T(8,128)(2,1)} copy(bf16[4096,3072]{1,0:T(8,128)(2,1)} %get-tuple-element.18) | data formatting | bytes 50331648
  (3 shorter events, 0.0 us)
Async XLA Ops:
  7.2 100.3 %all-gather.2.cloned.1.call-start = ((), (), s32[]{:S(2)}) async-start(), calls=%async_computation | async-start | bytes 21233664 | tf_op jit(solution)/shard_map/all_gather | solution.py:472
  14.5 2.8 copy-start
  17.2 1.7 copy-start.1
  64.7 1.7 copy-start.2
Sparse Core Ops, SparseCore 0:
  9.8 97.6 all-gather.1

commit v2 on v1

--- a/solution.py
+++ b/solution.py
@@ -21,45 +21,6 @@
     return (r % 2) * 4 + r // 2
 
 
-def _qkv_kernel(nb, x_ref, g_ref, c_ref, s_ref, wq_ref, wk_ref, wv_ref, q_ref, k_ref, v_ref, w, a, sems):
-    i = pl.program_id(0)
-    r = lax.axis_index("tp")
-    tm = x_ref.shape[0]
-    nq = wq_ref.shape[1]
-
-    @pl.when(i == 0)
-    def _():
-        col = pl.ds(pl.multiple_of(r * HEAD, HEAD), HEAD)
-        cps = [
-            pltpu.make_async_copy(wq_ref, w.at[:, pl.ds(0, nq)], sems.at[0]),
-            pltpu.make_async_copy(wk_ref.at[:, col], w.at[:, pl.ds(nq, HEAD)], sems.at[1]),
-            pltpu.make_async_copy(wv_ref.at[:, col], w.at[:, pl.ds(nq + HEAD, HEAD)], sems.at[2]),
-        ]
-        for cp in cps:
-            cp.start()
-        for cp in cps:
-            cp.wait()
-
-    _norm_rows(x_ref, g_ref, a, tm)
-    first = i < nb // 2
-    lane = lax.broadcasted_iota(jnp.int32, (tm, HEAD), 1)
-    low = lane < HEAD // 2
-    keep = jnp.logical_xor(low, jnp.logical_not(first))
-    cb, sb = c_ref[...], s_ref[...]
-    c = jnp.where(keep, cb, pltpu.roll(cb, HEAD // 2, 1))
-    s = jnp.where(keep, sb, pltpu.roll(sb, HEAD // 2, 1))
-    s = jnp.where(low, -s, s)
-    z = jnp.dot(a[...], w[...], preferred_element_type=F32)
-    for h in range(nq // HEAD + 1):
-        t = z[:, h * HEAD:(h + 1) * HEAD]
-        t = (t * c + pltpu.roll(t, HEAD // 2, 1) * s).astype(BF)
-        if h < nq // HEAD:
-            q_ref[:, h * HEAD:(h + 1) * HEAD] = t
-        else:
-            k_ref[...] = t
-    v_ref[...] = z[:, nq + HEAD:].astype(BF)
-
-
 def _norm_rows(src, g_ref, dst, rows, step=16):
     @pl.loop(0, rows // step, unroll=2)
     def _(n):
@@ -69,23 +30,23 @@
         dst[sl, :] = (t * inv * g_ref[...].astype(F32)).astype(BF)
 
 
-def _big_kernel(J, R, QB, x_ref, q_ref, k_ref, v_ref, wo_ref, g2_ref, wg_ref, wu_ref, wd_ref,
-                y_ref, oland, bland, rs1land,
+def _big_kernel(J, R, QB, x_ref, g1_ref, g2_ref, cos_ref, sin_ref, wq_ref, wk_ref, wv_ref, wo_ref, wg_ref, wu_ref,
+                wd_ref, y_ref, kout, vout, oland, bland, rs1land, woland,
                 wg, wu, wd, rs2x, rs2y, rs3a, rs3b, hk, own,
-                a2s, a2r, abs_, abr, ays, ayr, rss, rsr, lsem, wsem):
+                a2s, a2r, abs_, abr, ays, ayr, rss, rsr, wos, wor, lsem, wsem):
     me = lax.axis_index("tp")
     c, s = me // 2, me % 2
-    D = x_ref.shape[1]
+    T, D = x_ref.shape
     H = D // 2
-    T = x_ref.shape[0]
     C = 8 * R
     R4 = 4 * R
-    hq = q_ref.shape[1]
+    hq = wq_ref.shape[1]
+    nh = hq // HEAD
     cx = c + 1 - 2 * (c % 2)
     cy = (c + 2) % 4
     cd = 3 - c
     dev = lambda chip, core: chip * 2 + core
-    X, Y, PT = dev(cx, s), dev(cy, s), dev(c, 1 - s)
+    X, Y, DG, PT = dev(cx, s), dev(cy, s), dev(cd, s), dev(c, 1 - s)
     mypos = s * 4 + c
     px, py, pd = s * 4 + cx, s * 4 + cy, s * 4 + cd
 
@@ -100,6 +61,27 @@
     for m in range(1, 8):
         pl.semaphore_signal(bar, inc=1, device_id={"tp": (me + m) % 8}, device_id_type=MESH)
     pl.semaphore_wait(bar, 7)
+
+    W2 = hq // 2
+
+    def worows(d, off=0, n=hq):
+        return woland.at[pl.ds(pl.multiple_of(d * hq + off, W2), n), :]
+
+    def wo_copy(i):
+        k = dict(ss=wos.at[i], rs=wor.at[i])
+        if i < 3:
+            return rcopy(wo_ref, worows(me), to=(X, Y, PT)[i], **k)
+        d, off, n, to = ((X, 0, W2, Y), (Y, W2, W2, X), (X, 0, hq, PT), (Y, 0, hq, PT), (DG, 0, W2, PT),
+                         (DG, W2, W2, PT))[i - 3]
+        return rcopy(worows(d, off, n), worows(d, off, n), to=to, **k)
+
+    def wo_recv(i):
+        d = worows(*((X,), (Y,), (PT,), (DG, 0, W2), (DG, W2, W2), (dev(cx, 1 - s),), (dev(cy, 1 - s),),
+                     (dev(cd, 1 - s), 0, W2), (dev(cd, 1 - s), W2, W2))[i])
+        rcopy(d, d, wos.at[i], wor.at[i], PT).wait_recv()
+
+    wo_in = pltpu.make_async_copy(wo_ref, hk.at[pl.ds(0, hq), :], lsem.at[0, 0])
+    wo_out = pltpu.make_async_copy(hk.at[pl.ds(0, hq), :], worows(me), lsem.at[0, 0])
 
     def peer(m):
         return (me + m) % 8
@@ -116,50 +98,132 @@
     def a2a_land(j, m):
         return oland.at[pl.ds(pl.multiple_of(j * R, R), R), pl.ds(pl.multiple_of(frm(m) * hq, HEAD), hq)]
 
-    def attention(q, k, v, o, acc, mm, ll, asem):
-        cps = [pltpu.make_async_copy(q_ref, q, asem.at[0]), pltpu.make_async_copy(k_ref, k, asem.at[1]),
-               pltpu.make_async_copy(v_ref, v, asem.at[2])]
-        for cp in cps:
+    def a2a_own(j, o):
+        return pltpu.make_async_copy(o.at[pl.ds(pl.multiple_of(j * C + mypos * R, R), R), :], a2a_land(j, 0),
+                                     a2s.at[j, 0])
+
+    TM = min(512, T // 2)
+
+    def qkv(q, k, v, vt):
+        def run(w, xt, ct, st, tsem, msem):
+            nb = T // TM
+            col = pl.ds(pl.multiple_of(me * HEAD, HEAD), HEAD)
+            cps = [pltpu.make_async_copy(wq_ref, w.at[:, pl.ds(0, hq)], msem.at[0]),
+                   pltpu.make_async_copy(wk_ref.at[:, col], w.at[:, pl.ds(hq, HEAD)], msem.at[1]),
+                   pltpu.make_async_copy(wv_ref.at[:, col], w.at[:, pl.ds(hq + HEAD, HEAD)], msem.at[2])]
+
+            def tile(i, slot):
+                r = pl.ds(pl.multiple_of(i * TM, TM), TM)
+                t = pl.ds(pl.multiple_of((i % (nb // 2)) * TM, TM), TM)
+                return [pltpu.make_async_copy(x_ref.at[r, :], xt.at[slot], tsem.at[slot, 0]),
+                        pltpu.make_async_copy(cos_ref.at[t, :], ct.at[slot], tsem.at[slot, 1]),
+                        pltpu.make_async_copy(sin_ref.at[t, :], st.at[slot], tsem.at[slot, 2])]
+
+            for cp in tile(0, 0) + cps:
+                cp.start()
+            for i in range(3):
+                wo_copy(i).start()
+            wo_in.start()
+
+            @pl.loop(0, nb)
+            def _(i):
+                slot = i % 2
+
+                @pl.when(i + 1 < nb)
+                def _():
+                    for cp in tile(i + 1, 1 - slot):
+                        cp.start()
+
+                for cp in tile(i, slot):
+                    cp.wait()
+                _norm_rows(xt.at[slot], g1_ref, xt.at[slot], TM)
+
+                @pl.when(i == 0)
+                def _():
+                    for cp in cps:
+                        cp.wait()
+
+                row = pl.ds(pl.multiple_of(i * TM, TM), TM)
+                low = lax.broadcasted_iota(jnp.int32, (TM, HEAD), 1) < HEAD // 2
+                keep = jnp.logical_xor(low, i >= nb // 2)
+                cb, sb = ct[slot], st[slot]
+                cc = jnp.where(keep, cb, pltpu.roll(cb, HEAD // 2, 1))
+                ss = jnp.where(keep, sb, pltpu.roll(sb, HEAD // 2, 1))
+                ss = jnp.where(low, -ss, ss)
+                z = jnp.dot(xt[slot], w[...], preferred_element_type=F32)
+                for h in range(nh + 1):
+                    t = z[:, h * HEAD:(h + 1) * HEAD]
+                    t = (t * cc + pltpu.roll(t, HEAD // 2, 1) * ss).astype(BF)
+                    if h < nh:
+                        q[row, h * HEAD:(h + 1) * HEAD] = t
+                    else:
+                        k[row, :] = t
+                zv = z[:, hq + HEAD:]
+                v[row, :] = zv.astype(BF)
+                vt[:, row] = zv.T.astype(BF)
+
+        pl.run_scoped(run, pltpu.VMEM((D, hq + 2 * HEAD), BF), pltpu.VMEM((2, TM, D), BF),
+                      pltpu.VMEM((2, TM, HEAD), F32), pltpu.VMEM((2, TM, HEAD), F32),
+                      pltpu.SemaphoreType.DMA((2, 3)), pltpu.SemaphoreType.DMA((3,)))
+
+    def attention(q, k, v, vt, acc, mm, ll, mx, sb, asem):
+        qkv(q, k, v, vt)
+        kv_out = [pltpu.make_async_copy(k, kout, asem.at[0]), pltpu.make_async_copy(v, vout, asem.at[1])]
+        for cp in kv_out + wcp:
             cp.start()
-        for cp in wcp:
-            cp.start()
-        for cp in cps:
-            cp.wait()
-        nh = hq // HEAD
+        wo_in.wait()
+        wo_out.start()
         sc = (HEAD ** -0.5) * LOG2E
-
-        def block(row, kb, masked):
-            kv = pl.ds(pl.multiple_of(kb * QB, QB), QB)
-            kk, vv = k[kv, :], v[kv, :]
-            for h in range(nh):
-                qq = q[row, h * HEAD:(h + 1) * HEAD]
-                sco = lax.dot_general(qq, kk, (((1,), (1,)), ((), ())), preferred_element_type=F32) * sc
-                if masked:
-                    ri = lax.broadcasted_iota(jnp.int32, (QB, QB), 0)
-                    ci = lax.broadcasted_iota(jnp.int32, (QB, QB), 1)
-                    sco = jnp.where(ci <= ri, sco, -jnp.inf)
-                mo = mm[h, :, :1]
-                mn = jnp.maximum(mo, jnp.max(sco, axis=-1, keepdims=True))
-                al = jnp.exp2(mo - mn)
-                p = jnp.exp2(sco - mn)
-                ll[h] = ll[h] * al + jnp.sum(p, axis=-1, keepdims=True)
-                acc[h] = acc[h] * al + jnp.dot(p.astype(BF), vv, preferred_element_type=F32)
-                mm[h] = jnp.broadcast_to(mn, (QB, HEAD))
-
-        @pl.loop(0, T // QB)
+        nq = T // QB
+        ki = lax.broadcasted_iota(jnp.int32, (QB, QB), 0)
+        qi = lax.broadcasted_iota(jnp.int32, (QB, QB), 1)
+
+        @pl.loop(0, nq)
         def _(i):
             row = pl.ds(pl.multiple_of(i * QB, QB), QB)
+
+            def qk(kb, h, masked=False):
+                kk = k[pl.ds(pl.multiple_of(kb * QB, QB), QB), :]
+                t = lax.dot_general(kk, q[row, h * HEAD:(h + 1) * HEAD], (((1,), (1,)), ((), ())),
+                                    preferred_element_type=F32)
+                if masked:
+                    t = jnp.where(ki <= qi, t, -jnp.inf)
+                sb[h] = t
+                mx[h] = jnp.max(t, axis=0, keepdims=True)
+
+            def soft(kb, h):
+                mo = mm[h]
+                mn = jnp.maximum(mo, mx[h])
+                mm[h] = mn
+                al = jnp.exp2((mo - mn) * sc)
+                p = jnp.exp2((sb[h] - mn) * sc)
+                ll[h] = ll[h] * al + jnp.sum(p, axis=0, keepdims=True)
+                acc[h] = acc[h] * al + jnp.dot(vt[:, pl.ds(pl.multiple_of(kb * QB, QB), QB)], p.astype(BF),
+                                               preferred_element_type=F32)
+
             acc[...] = jnp.zeros_like(acc)
             ll[...] = jnp.zeros_like(ll)
             mm[...] = jnp.full_like(mm, -jnp.inf)
 
+            def phases(kb, nxt, masked):
+                for h in range(nh):
+                    ahead = h + nh - 1
+                    if ahead < nh:
+                        qk(kb, ahead, masked)
+                    else:
+                        qk(nxt, ahead - nh)
+                    soft(kb, h)
+
+            for h in range(nh - 1):
+                qk(i, h, True)
+            phases(i, 0, True)
+
             @pl.loop(0, i)
             def _(kb):
-                block(row, kb, False)
-
-            block(row, i, True)
+                phases(kb, kb + 1, False)
+
             for h in range(nh):
-                o[row, h * HEAD:(h + 1) * HEAD] = (acc[h] / ll[h]).astype(BF)
+                q[row, h * HEAD:(h + 1) * HEAD] = (acc[h] / ll[h]).T.astype(BF)
 
             per = C // QB
 
@@ -167,25 +231,38 @@
             def _():
                 j = i // per
                 for m in range(1, 8):
-                    a2a(j, m, o).start()
-                pltpu.make_async_copy(
-                    o.at[pl.ds(pl.multiple_of(j * C + mypos * R, R), R), :],
-                    oland.at[pl.ds(pl.multiple_of(j * R, R), R), pl.ds(pl.multiple_of(me * hq, HEAD), hq)],
-                    a2s.at[j, 0]).start()
+                    a2a(j, m, q).start()
+                a2a_own(j, q).start()
+
+            @pl.when(i == nq // 2)
+            def _():
+                for n in (0, 1):
+                    wo_recv(n)
+                    wo_copy(n + 3).start()
+                for n in (5, 6):
+                    wo_copy(n).start()
+
+        for n in (3, 4):
+            wo_recv(n)
+            wo_copy(n + 4).start()
+        for cp in kv_out:
+            cp.wait()
 
         @pl.loop(0, J)
         def _(j):
-            pltpu.make_async_copy(
-                o.at[pl.ds(pl.multiple_of(j * C + mypos * R, R), R), :],
-                oland.at[pl.ds(pl.multiple_of(j * R, R), R), pl.ds(pl.multiple_of(me * hq, HEAD), hq)],
-                a2s.at[j, 0]).wait()
+            a2a_own(j, q).wait()
             for m in range(1, 8):
-                a2a(j, m, o).wait_send()
+                a2a(j, m, q).wait_send()
 
     pl.run_scoped(attention, pltpu.VMEM((T, hq), BF), pltpu.VMEM((T, HEAD), BF), pltpu.VMEM((T, HEAD), BF),
-                  pltpu.VMEM((T, hq), BF), pltpu.VMEM((hq // HEAD, QB, HEAD), F32),
-                  pltpu.VMEM((hq // HEAD, QB, HEAD), F32), pltpu.VMEM((hq // HEAD, QB, HEAD), F32),
-                  pltpu.SemaphoreType.DMA((3,)))
+                  pltpu.VMEM((HEAD, T), BF), pltpu.VMEM((nh, HEAD, QB), F32),
+                  pltpu.VMEM((nh, 1, QB), F32), pltpu.VMEM((nh, 1, QB), F32), pltpu.VMEM((nh, 1, QB), F32),
+                  pltpu.VMEM((nh, QB, QB), F32), pltpu.SemaphoreType.DMA((2,)))
+    wo_out.wait()
+    for n in (2, 5, 6, 7, 8):
+        wo_recv(n)
+    for n in range(9):
+        wo_copy(n).wait_send()
 
     NT = min(512, D)
 
@@ -195,7 +272,7 @@
                                   hk.at[pl.ds(j * R, R), :], osem.at[1 + j]).start()
 
         def tile(n, slot):
-            return pltpu.make_async_copy(wo_ref.at[:, pl.ds(pl.multiple_of(n * NT, NT), NT)], wt.at[slot],
+            return pltpu.make_async_copy(woland.at[:, pl.ds(pl.multiple_of(n * NT, NT), NT)], wt.at[slot],
                                          tsem.at[slot])
 
         tile(0, 0).start()
@@ -469,49 +546,30 @@
         t, d = x.shape
         hq = wq.shape[1]
         ff = wg.shape[1]
-        wo_full = lax.all_gather(wo, "tp", axis=0, tiled=True)
         cs, sn = _tables(pos)
-        tm = min(512, t // 2)
-        nb = t // tm
-        row = lambda i: (i, 0)
-        q, k, v = pl.pallas_call(
-            functools.partial(_qkv_kernel, nb),
-            grid=(nb,),
-            in_specs=[pl.BlockSpec((tm, d), row), pl.BlockSpec((1, d), lambda i: (0, 0)),
-                      pl.BlockSpec((tm, HEAD), lambda i: (i % (nb // 2), 0)),
-                      pl.BlockSpec((tm, HEAD), lambda i: (i % (nb // 2), 0)), ANY, ANY, ANY],
-            out_specs=[pl.BlockSpec((tm, hq), row), pl.BlockSpec((tm, HEAD), row), pl.BlockSpec((tm, HEAD), row)],
-            out_shape=[jax.ShapeDtypeStruct((t, hq), BF), jax.ShapeDtypeStruct((t, HEAD), BF),
-                       jax.ShapeDtypeStruct((t, HEAD), BF)],
-            scratch_shapes=[pltpu.VMEM((d, hq + 2 * HEAD), BF), pltpu.VMEM((tm, d), BF),
-                            pltpu.SemaphoreType.DMA((3,))],
-            compiler_params=pltpu.CompilerParams(dimension_semantics=("arbitrary",), vmem_limit_bytes=40 << 20),
-            cost_estimate=pl.CostEstimate(flops=2 * t * d * (hq + 2 * HEAD), bytes_accessed=2 * t * d,
-                                          transcendentals=0),
-            name="qkv",
-        )(x, g1.reshape(1, d), cs, sn, wq, wk, wv)
-
         J = NCHUNK
         R = t // 8 // J
         QB = min(512, 8 * R)
         dma = pltpu.SemaphoreType.DMA
-        y, _, _, _ = pl.pallas_call(
+        vm = pl.BlockSpec(memory_space=pltpu.VMEM)
+        big = lambda *sh: jax.ShapeDtypeStruct(sh, BF)
+        y, k, v, *_ = pl.pallas_call(
             functools.partial(_big_kernel, J, R, QB),
-            in_specs=[ANY] * 5 + [pl.BlockSpec(memory_space=pltpu.VMEM)] + [ANY] * 3,
-            out_specs=[ANY] * 4,
-            out_shape=[jax.ShapeDtypeStruct((t, d), BF), jax.ShapeDtypeStruct((J * R, 8 * hq), BF),
-                       jax.ShapeDtypeStruct((t, d), BF), jax.ShapeDtypeStruct((J, 4 * R, d), BF)],
+            in_specs=[ANY, vm, vm] + [ANY] * 9,
+            out_specs=[ANY] * 7,
+            out_shape=[big(t, d), big(t, HEAD), big(t, HEAD), big(J * R, 8 * hq), big(t, d), big(J, 4 * R, d),
+                       big(8 * hq, d)],
             scratch_shapes=[pltpu.VMEM((d, ff), BF), pltpu.VMEM((d, ff), BF), pltpu.VMEM((ff, d), BF),
                             pltpu.VMEM((J, 2, R, d // 2), BF), pltpu.VMEM((J, 2, R, d // 2), BF),
                             pltpu.VMEM((J, R, d // 2), BF), pltpu.VMEM((J, R, d // 2), BF),
                             pltpu.VMEM((J * R, d), BF), pltpu.VMEM((J * R, d), BF),
                             dma((J, 8)), dma((J, 8)), dma((J, 9)), dma((J, 9)), dma((J, 9)), dma((J, 9)),
-                            dma((J, 7)), dma((J, 7)), dma((2, J)), dma((3,))],
+                            dma((J, 7)), dma((J, 7)), dma((9,)), dma((9,)), dma((2, J)), dma((3,))],
             compiler_params=pltpu.CompilerParams(collective_id=0, has_side_effects=True,
                                                  vmem_limit_bytes=67043328),
-            cost_estimate=pl.CostEstimate(flops=2 * t * d * ff * 3, bytes_accessed=2 * t * d * 6, transcendentals=0),
+            cost_estimate=pl.CostEstimate(flops=2 * t * d * ff * 4, bytes_accessed=2 * t * d * 6, transcendentals=0),
             name="layer",
-        )(x, q, k, v, wo_full, g2.reshape(1, d), wg, wu, wd)
+        )(x, g1.reshape(1, d), g2.reshape(1, d), cs, sn, wq, wk, wv, wo, wg, wu, wd)
         return y, k.reshape(t, 1, HEAD), v.reshape(t, 1, HEAD)
 
     return jax.shard_map(

time: 634 us -> 511 us (0.81)
  Pallas kernels: 544 us -> 478 us
  waiting for transfers between devices: 41.8 us -> 0 us
  between operations: 14.1 us -> 0.67 us
    pallas_call x2 -> x1, Pallas kernels: 544 us -> 478 us  [local(): pl.pallas_call(functools.partial(_big_kernel, J, R, QB), in_specs=[ANY, v...]
    all_gather x1 -> x0, waiting for transfers between devices: 41.1 us -> none  [local(): wo_full = lax.all_gather(wo, 'tp', axis=0, tiled=True)]
  transfers between devices with their start and end apart: 1 -> 0, of which waited for: 1 -> 0; matrix products, arithmetic and copies ran while one was open for 1% -> 0% of each run, Pallas kernels for 7% -> 0%
where the time goes in v2:
time: 511 us; the launch traced here: 510 us
  Pallas kernels  478 us (94%)
  local copies, waits for them, and re-layouts  25.4 us (5%)
  other arithmetic  6.36 us (1%)
    pallas_call x1, Pallas kernels, local(): pl.pallas_call(functools.partial(_big_kernel, J, R, QB), in_specs=[ANY, v...  478 us
    unnamed x7, local copies, waits for them, and re-layouts  22.8 us

profile of v2, /device:TPU:0, one launch (start us, length us, event | category | flops | bytes accessed | tf_op | source)
XLA Modules:
  0.0 510.3 jit_solution(18127084323570494955)
XLA Ops:
  0.7 0.1 pad_maximum_fusion
  0.7 1.3 reshape.21.g1_ref
  2.0 1.3 reshape.22.g2_ref
  3.3 0.7 convert_element_type.3
  4.1 5.5 %fusion = (f32[2048,128]{1,0:T(8,128)}, f32[2048,128]{1,0:T(8,128)}) fusion(f32[128]{0:T(128)S(1)} %pad_maximum_fusion, f32[2048]{0:T(1024)S(1)} %get-tuple-element.12, f32[2048]{0:T(1024)S(1)} %get-tuple-element.11, pred[128]{0:T(512)(128)(4,1)S(1)} %iota_compare_fusion), kind=kLoop, calls=%fused_computation.1 | loop fusion | flops 524288 | bytes 2114176 | tf_op jit(solution)/shard_map/sin | solution.py:541
  9.6 477.9 %layer.1 = (bf16[4096,3072]{1,0:T(8,128)(2,1)}, bf16[4096,128]{1,0:T(8,128)(2,1)}, bf16[4096,128]{1,0:T(8,128)(2,1)}, bf16[512,3072]{1,0:T(8,128)(2,1)}, bf16[40...) custom-call(bf16[4096,3072]{1,0:T(8,128)(2,1)} %x_ref.1, ...), custom_call_target="tpu_custom_call" | custom-call | flops 103079215104 | bytes 150994944 | tf_op jit(solution)/shard_map/layer/pallas_call | solution.py:556
  487.5 0.0 copy-start.1
  487.5 0.0 copy-start
  487.5 20.8 %copy.17 = bf16[4096,3072]{1,0:T(8,128)(2,1)} copy(bf16[4096,3072]{1,0:T(8,128)(2,1)} %get-tuple-element.16) | data formatting | bytes 50331648
  508.3 0.0 copy-done.1
  508.3 1.0 copy.18
  509.3 0.0 copy-done
  509.3 1.0 copy.19
  (3 shorter events, 0.0 us)
Async XLA Ops:
  487.5 20.8 %copy-start.1 = (bf16[4096,128]{1,0:T(8,128)(2,1)S(1)}, bf16[4096,128]{1,0:T(8,128)(2,1)}, u32[]{:S(2)}) copy-start(bf16[4096,128]{1,0:T(8,128)(2,1)} %get-tuple-element.7) | copy-start | bytes 3145732
  487.5 21.8 %copy-start = (bf16[4096,128]{1,0:T(8,128)(2,1)S(1)}, bf16[4096,128]{1,0:T(8,128)(2,1)}, u32[]{:S(2)}) copy-start(bf16[4096,128]{1,0:T(8,128)(2,1)} %get-tuple-element.8) | copy-start | bytes 3145732

commit v3 on v2

--- a/solution.py
+++ b/solution.py
@@ -11,7 +11,7 @@
 EPS = 1e-5
 ROPE_BASE = 500000.0
 LOG2E = 1.4426950408889634
-NCHUNK = 4
+NCHUNK = 8
 MESH = pl.DeviceIdType.MESH
 F32, BF = jnp.float32, jnp.bfloat16
 ANY = pl.BlockSpec(memory_space=pl.ANY)

time: 511 us -> 508 us (level)
  no operation moved by 1% of the time
where the time goes in v3:
time: 508 us; the launch traced here: 507 us
  Pallas kernels  474 us (93%)
  local copies, waits for them, and re-layouts  25.4 us (5%)
  other arithmetic  6.36 us (1%)
    pallas_call x1, Pallas kernels, local(): pl.pallas_call(functools.partial(_big_kernel, J, R, QB), in_specs=[ANY, v...  474 us
    unnamed x7, local copies, waits for them, and re-layouts  22.8 us

profile of v3, /device:TPU:0, one launch (start us, length us, event | category | flops | bytes accessed | tf_op | source)
XLA Modules:
  0.0 506.9 jit_solution(16083028083789150153)
XLA Ops:
  0.7 0.1 pad_maximum_fusion
  0.7 1.3 reshape.21.g1_ref
  2.0 1.3 reshape.22.g2_ref
  3.3 0.7 convert_element_type.3
  4.1 5.5 %fusion = (f32[2048,128]{1,0:T(8,128)}, f32[2048,128]{1,0:T(8,128)}) fusion(f32[128]{0:T(128)S(1)} %pad_maximum_fusion, f32[2048]{0:T(1024)S(1)} %get-tuple-element.12, f32[2048]{0:T(1024)S(1)} %get-tuple-element.11, pred[128]{0:T(512)(128)(4,1)S(1)} %iota_compare_fusion), kind=kLoop, calls=%fused_computation.1 | loop fusion | flops 524288 | bytes 2114176 | tf_op jit(solution)/shard_map/sin | solution.py:541
  9.6 474.5 %layer.1 = (bf16[4096,3072]{1,0:T(8,128)(2,1)}, bf16[4096,128]{1,0:T(8,128)(2,1)}, bf16[4096,128]{1,0:T(8,128)(2,1)}, bf16[512,3072]{1,0:T(8,128)(2,1)}, bf16[40...) custom-call(bf16[4096,3072]{1,0:T(8,128)(2,1)} %x_ref.1, ...), custom_call_target="tpu_custom_call" | custom-call | flops 103079215104 | bytes 150994944 | tf_op jit(solution)/shard_map/layer/pallas_call | solution.py:556
  484.1 0.0 copy-start.1
  484.1 0.0 copy-start
  484.1 20.8 %copy.17 = bf16[4096,3072]{1,0:T(8,128)(2,1)} copy(bf16[4096,3072]{1,0:T(8,128)(2,1)} %get-tuple-element.16) | data formatting | bytes 50331648
  504.9 0.0 copy-done.1
  504.9 1.0 copy.18
  505.9 0.0 copy-done
  505.9 1.0 copy.19
  (3 shorter events, 0.0 us)
Async XLA Ops:
  484.1 20.8 %copy-start.1 = (bf16[4096,128]{1,0:T(8,128)(2,1)S(1)}, bf16[4096,128]{1,0:T(8,128)(2,1)}, u32[]{:S(2)}) copy-start(bf16[4096,128]{1,0:T(8,128)(2,1)} %get-tuple-element.7) | copy-start | bytes 3145732
  484.1 21.8 %copy-start = (bf16[4096,128]{1,0:T(8,128)(2,1)S(1)}, bf16[4096,128]{1,0:T(8,128)(2,1)}, u32[]{:S(2)}) copy-start(bf16[4096,128]{1,0:T(8,128)(2,1)} %get-tuple-element.8) | copy-start | bytes 3145732

commit v4 on v3

--- a/solution.py
+++ b/solution.py
@@ -28,6 +28,10 @@
         t = src[sl, :].astype(F32)
         inv = lax.rsqrt(jnp.mean(t * t, axis=-1, keepdims=True) + EPS)
         dst[sl, :] = (t * inv * g_ref[...].astype(F32)).astype(BF)
+
+
+def _copy_kernel(i_ref, o_ref):
+    o_ref[...] = i_ref[...]
 
 
 def _big_kernel(J, R, QB, x_ref, g1_ref, g2_ref, cos_ref, sin_ref, wq_ref, wk_ref, wv_ref, wo_ref, wg_ref, wu_ref,
@@ -264,52 +268,6 @@
     for n in range(9):
         wo_copy(n).wait_send()
 
-    NT = min(512, D)
-
-    def oproj(oo, wt, osem, tsem):
-        for j in range(J):
-            pltpu.make_async_copy(x_ref.at[pl.ds(pl.multiple_of(j * C + mypos * R, R), R), :],
-                                  hk.at[pl.ds(j * R, R), :], osem.at[1 + j]).start()
-
-        def tile(n, slot):
-            return pltpu.make_async_copy(woland.at[:, pl.ds(pl.multiple_of(n * NT, NT), NT)], wt.at[slot],
-                                         tsem.at[slot])
-
-        tile(0, 0).start()
-
-        @pl.loop(0, J)
-        def _(j):
-            for m in range(1, 8):
-                pltpu.make_async_remote_copy(src_ref=a2a_land(j, m), dst_ref=a2a_land(j, m), send_sem=a2s.at[j, m],
-                                             recv_sem=a2r.at[j, m], device_id={"tp": frm(m)},
-                                             device_id_type=MESH).wait_recv()
-
-        cp = pltpu.make_async_copy(oland, oo, osem.at[0])
-        cp.start()
-        cp.wait()
-        for j in range(J):
-            pltpu.make_async_copy(x_ref.at[pl.ds(pl.multiple_of(j * C + mypos * R, R), R), :],
-                                  hk.at[pl.ds(j * R, R), :], osem.at[1 + j]).wait()
-        nt = D // NT
-
-        @pl.loop(0, nt)
-        def _(n):
-            slot = n % 2
-
-            @pl.when(n + 1 < nt)
-            def _():
-                tile(n + 1, 1 - slot).start()
-
-            tile(n, slot).wait()
-            col = pl.ds(pl.multiple_of(n * NT, NT), NT)
-            hk[:, col] = (hk[:, col].astype(F32)
-                          + jnp.dot(oo[...], wt[slot], preferred_element_type=F32)).astype(BF)
-
-        _norm_rows(hk, g2_ref, own, J * R)
-
-    pl.run_scoped(oproj, pltpu.VMEM((J * R, 8 * hq), BF), pltpu.VMEM((2, 8 * hq, NT), BF), pltpu.SemaphoreType.DMA((1 + J,)),
-                  pltpu.SemaphoreType.DMA((2,)))
-
     R2 = R // 2
 
     def rows(land, j, pos, off=0, n=R):
@@ -373,7 +331,52 @@
         def _(i):
             f(pl.ds(pl.multiple_of(i * 16, 16), 16))
 
-    def mlp(bt, us, pb, rt, sums, bsem):
+    def mlp(bt, us, pb, rt, sums, oo, wt, bsem, osem, tsem):
+        NT = wt.shape[2]
+        JH = J // 2
+        RH = JH * R
+
+        def x_in(j):
+            return pltpu.make_async_copy(x_ref.at[pl.ds(pl.multiple_of(j * C + mypos * R, R), R), :],
+                                         hk.at[pl.ds(pl.multiple_of(j * R, R), R), :], osem.at[1 + j])
+
+        def oproj(half):
+            part = pl.ds(half * RH, RH)
+
+            def tile(n, slot):
+                return pltpu.make_async_copy(woland.at[:, pl.ds(pl.multiple_of(n * NT, NT), NT)], wt.at[slot],
+                                             tsem.at[slot])
+
+            tile(0, 0).start()
+
+            @pl.loop(half * JH, (half + 1) * JH)
+            def _(j):
+                for m in range(1, 8):
+                    d = a2a_land(j, m)
+                    rcopy(d, d, a2s.at[j, m], a2r.at[j, m], PT).wait_recv()
+
+            cp = pltpu.make_async_copy(oland.at[part, :], oo, osem.at[0])
+            cp.start()
+            cp.wait()
+            for j in range(half * JH, (half + 1) * JH):
+                x_in(j).wait()
+            nt = D // NT
+
+            @pl.loop(0, nt)
+            def _(n):
+                slot = n % 2
+
+                @pl.when(n + 1 < nt)
+                def _():
+                    tile(n + 1, 1 - slot).start()
+
+                tile(n, slot).wait()
+                col = pl.ds(pl.multiple_of(n * NT, NT), NT)
+                hk[part, col] = (hk[part, col].astype(F32)
+                                 + jnp.dot(oo[...], wt[slot], preferred_element_type=F32)).astype(BF)
+
+            _norm_rows(hk.at[part, :], g2_ref, own.at[part, :], RH)
+
         def sumsl(j, chip, col):
             return sums.at[j % 2, pl.ds(pl.multiple_of(chip * R, R), R), col]
 
@@ -396,13 +399,11 @@
             return rcopy(sumsl(j, cx, hi), rs3b.at[j], to=X, **k)
 
         def load_b(j, half):
-            pos = jnp.where(half == 0, 1 - s, s) * 4 if not isinstance(half, int) else ((1 - s) if half == 0 else s) * 4
+            pos = ((1 - s) if half == 0 else s) * 4
             return pltpu.make_async_copy(bland.at[pl.ds(pl.multiple_of(j * C + pos * R, R4), R4), :], bt.at[half],
                                          bsem.at[half])
 
         def compute(j):
-            for half in range(2):
-                load_b(j, half).start()
             for half in range(2):
                 load_b(j, half).wait()
                 if half == 0:
@@ -426,7 +427,7 @@
                     rs_copy(j, 0).start()
 
             rs_copy(j, 0).wait_recv()
-            cp = pltpu.make_async_copy(rs1land.at[j], rt, bsem.at[0])
+            cp = pltpu.make_async_copy(rs1land.at[j], rt, bsem.at[2])
             cp.start()
             cp.wait()
 
@@ -472,45 +473,56 @@
             ew(R, fin)
             g_own(*gy, j, 1)
 
+        for j in range(J):
+            x_in(j).start()
+        oproj(0)
         g_own(*gb, 0, 0)
         for cp in wcp:
             cp.wait()
-
-        @pl.loop(0, J + 2)
+        oproj(1)
+        g_fwd(*gb, 0)
+        g_own(*gb, 1, 0)
+
+        @pl.loop(0, J + 4)
         def _(t):
             @pl.when(t < J)
             def _():
-                g_fwd(*gb, t)
-
-            @pl.when(jnp.logical_and(t >= 1, t <= J))
-            def _():
-                rs3(t - 1)
-
-            @pl.when(t >= 2)
-            def _():
-                g_fwd(*gy, t - 2)
+                g_fwd2(*gb, t)
 
             @pl.when(t + 1 < J)
             def _():
-                g_own(*gb, t + 1, 0)
-
-            @pl.when(t < J)
-            def _():
-                g_fwd2(*gb, t)
-
-            @pl.when(jnp.logical_and(t >= 1, t <= J))
-            def _():
-                final(t - 1)
+                g_fwd(*gb, t + 1)
+
+            @pl.when(t >= 4)
+            def _():
+                g_fwd2(*gy, t - 4)
+
+            @pl.when(jnp.logical_and(t >= 3, t < J + 3))
+            def _():
+                g_fwd(*gy, t - 3)
+
+            @pl.when(t + 2 < J)
+            def _():
+                g_own(*gb, t + 2, 0)
 
             @pl.when(t < J)
             def _():
                 g_finish(*gb, t)
                 g_local(bland, t, 0).wait()
+                for half in range(2):
+                    load_b(t, half).start()
+
+            @pl.when(jnp.logical_and(t >= 2, t < J + 2))
+            def _():
+                final(t - 2)
+
+            @pl.when(t < J)
+            def _():
                 compute(t)
 
-            @pl.when(t >= 2)
-            def _():
-                g_fwd2(*gy, t - 2)
+            @pl.when(jnp.logical_and(t >= 1, t < J + 1))
+            def _():
+                rs3(t - 1)
 
         rs_copy(J - 1, 0).wait_send()
         for j in range(max(J - 2, 0), J):
@@ -518,7 +530,9 @@
                 rs_copy(j, i).wait_send()
 
     pl.run_scoped(mlp, pltpu.VMEM((2, R4, D), BF), pltpu.VMEM((R4, wg.shape[1]), BF), pltpu.VMEM((2, R4, D), BF),
-                  pltpu.VMEM((R4, D), BF), pltpu.VMEM((2, R4, D), BF), pltpu.SemaphoreType.DMA((2,)))
+                  pltpu.VMEM((R4, D), BF), pltpu.VMEM((2, R4, D), BF), pltpu.VMEM((J * R // 2, 8 * hq), BF),
+                  pltpu.VMEM((2, 8 * hq, min(512, D)), BF), pltpu.SemaphoreType.DMA((3,)),
+                  pltpu.SemaphoreType.DMA((1 + J,)), pltpu.SemaphoreType.DMA((2,)))
 
     @pl.loop(0, J)
     def _(j):
@@ -570,6 +584,10 @@
             cost_estimate=pl.CostEstimate(flops=2 * t * d * ff * 4, bytes_accessed=2 * t * d * 6, transcendentals=0),
             name="layer",
         )(x, g1.reshape(1, d), g2.reshape(1, d), cs, sn, wq, wk, wv, wo, wg, wu, wd)
+        cb = pl.BlockSpec((min(256, t), d), lambda i: (i, 0))
+        y = pl.pallas_call(_copy_kernel, grid=(t // min(256, t),), in_specs=[cb], out_specs=cb, out_shape=big(t, d),
+                           compiler_params=pltpu.CompilerParams(dimension_semantics=("arbitrary",)),
+                           name="out")(y)
         return y, k.reshape(t, 1, HEAD), v.reshape(t, 1, HEAD)
 
     return jax.shard_map(

time: 508 us -> 497 us (0.978)
  local copies, waits for them, and re-layouts: 25.4 us -> 4.55 us
  Pallas kernels: 474 us -> 484 us
    pallas_call x0 -> x1, Pallas kernels: none -> 22.4 us  [local(): pl.pallas_call(_copy_kernel, grid=(t // min(256, t),), in_specs=[cb], out...]
    unnamed x7 -> x6, local copies, waits for them, and re-layouts: 22.8 us -> 1.95 us
    pallas_call x1, Pallas kernels: 474 us -> 462 us  [local(): pl.pallas_call(functools.partial(_big_kernel, J, R, QB), in_specs=[ANY, v...]
where the time goes in v4:
time: 497 us; the launch traced here: 496 us
  Pallas kernels  484 us (97%)
  other arithmetic  6.36 us (1%)
    pallas_call x1, Pallas kernels, local(): pl.pallas_call(functools.partial(_big_kernel, J, R, QB), in_specs=[ANY, v...  462 us
    pallas_call x1, Pallas kernels, local(): pl.pallas_call(_copy_kernel, grid=(t // min(256, t),), in_specs=[cb], out...  22.4 us

profile of v4, /device:TPU:0, one launch (start us, length us, event | category | flops | bytes accessed | tf_op | source)
XLA Modules:
  0.0 495.7 jit_solution(2712341203736325289)
XLA Ops:
  0.7 0.1 pad_maximum_fusion
  0.7 1.3 reshape.21.g1_ref
  2.0 1.3 reshape.22.g2_ref
  3.3 0.7 convert_element_type.3
  4.1 5.5 %fusion = (f32[2048,128]{1,0:T(8,128)}, f32[2048,128]{1,0:T(8,128)}) fusion(f32[128]{0:T(128)S(1)} %pad_maximum_fusion, f32[2048]{0:T(1024)S(1)} %get-tuple-element.12, f32[2048]{0:T(1024)S(1)} %get-tuple-element.11, pred[128]{0:T(512)(128)(4,1)S(1)} %iota_compare_fusion), kind=kLoop, calls=%fused_computation.1 | loop fusion | flops 524288 | bytes 2114176 | tf_op jit(solution)/shard_map/sin | solution.py:555
  9.6 461.7 %layer.1 = (bf16[4096,3072]{1,0:T(8,128)(2,1)}, bf16[4096,128]{1,0:T(8,128)(2,1)}, bf16[4096,128]{1,0:T(8,128)(2,1)}, bf16[512,3072]{1,0:T(8,128)(2,1)}, bf16[40...) custom-call(bf16[4096,3072]{1,0:T(8,128)(2,1)} %x_ref.1, ...), custom_call_target="tpu_custom_call" | custom-call | flops 103079215104 | bytes 150994944 | tf_op jit(solution)/shard_map/layer/pallas_call | solution.py:570
  471.3 0.0 copy-start.1
  471.3 0.0 copy-start
  471.3 22.4 %out.1 = bf16[4096,3072]{1,0:T(8,128)(2,1)} custom-call(bf16[4096,3072]{1,0:T(8,128)(2,1)} %get-tuple-element.6.i_ref), custom_call_target="tpu_custom_call" | custom-call | tf_op jit(solution)/shard_map/out/pallas_call | solution.py:588
  493.7 0.0 copy-done.1
  493.7 1.0 copy.16
  494.7 0.0 copy-done
  494.7 1.0 copy.17
  (3 shorter events, 0.0 us)
Async XLA Ops:
  471.3 22.4 %copy-start.1 = (bf16[4096,128]{1,0:T(8,128)(2,1)S(1)}, bf16[4096,128]{1,0:T(8,128)(2,1)}, u32[]{:S(2)}) copy-start(bf16[4096,128]{1,0:T(8,128)(2,1)} %get-tuple-element.7) | copy-start | bytes 3145732
  471.3 23.4 %copy-start = (bf16[4096,128]{1,0:T(8,128)(2,1)S(1)}, bf16[4096,128]{1,0:T(8,128)(2,1)}, u32[]{:S(2)}) copy-start(bf16[4096,128]{1,0:T(8,128)(2,1)} %get-tuple-element.8) | copy-start | bytes 3145732

commit v5 on v4

--- a/solution.py
+++ b/solution.py
@@ -30,8 +30,23 @@
         dst[sl, :] = (t * inv * g_ref[...].astype(F32)).astype(BF)
 
 
-def _copy_kernel(i_ref, o_ref):
-    o_ref[...] = i_ref[...]
+def _copy_kernel(nt, y, k, v, yo, ko, vo, yb, kb, vb, si, so):
+    rows = y.shape[0] // nt
+    ins, outs = [], []
+    for i in range(nt):
+        r = pl.ds(i * rows, rows)
+        ins.append(pltpu.make_async_copy(y.at[r, :], yb.at[r, :], si.at[i]))
+        outs.append(pltpu.make_async_copy(yb.at[r, :], yo.at[r, :], so.at[i]))
+    for i, (a, b, o) in enumerate(((k, kb, ko), (v, vb, vo))):
+        ins.append(pltpu.make_async_copy(a, b, si.at[nt + i]))
+        outs.append(pltpu.make_async_copy(b, o, so.at[nt + i]))
+    for cp in ins:
+        cp.start()
+    for a, b in zip(ins, outs):
+        a.wait()
+        b.start()
+    for cp in outs:
+        cp.wait()
 
 
 def _big_kernel(J, R, QB, x_ref, g1_ref, g2_ref, cos_ref, sin_ref, wq_ref, wk_ref, wv_ref, wo_ref, wg_ref, wu_ref,
@@ -54,9 +69,12 @@
     mypos = s * 4 + c
     px, py, pd = s * 4 + cx, s * 4 + cy, s * 4 + cd
 
+    z = lax.axis_index("dp")
+
     def rcopy(src, dst, ss, rs, to):
+        where = {"dp": 1 - z, "tp": me} if to is None else {"tp": to}
         return pltpu.make_async_remote_copy(src_ref=src, dst_ref=dst, send_sem=ss, recv_sem=rs,
-                                            device_id={"tp": to}, device_id_type=MESH)
+                                            device_id=where, device_id_type=MESH)
 
     wcp = [pltpu.make_async_copy(wg_ref, wg, wsem.at[0]), pltpu.make_async_copy(wu_ref, wu, wsem.at[1]),
            pltpu.make_async_copy(wd_ref, wd, wsem.at[2])]
@@ -64,28 +82,41 @@
     bar = pltpu.get_barrier_semaphore()
     for m in range(1, 8):
         pl.semaphore_signal(bar, inc=1, device_id={"tp": (me + m) % 8}, device_id_type=MESH)
-    pl.semaphore_wait(bar, 7)
-
-    W2 = hq // 2
-
-    def worows(d, off=0, n=hq):
-        return woland.at[pl.ds(pl.multiple_of(d * hq + off, W2), n), :]
+    pl.semaphore_signal(bar, inc=1, device_id={"dp": 1 - z, "tp": me}, device_id_type=MESH)
+    pl.semaphore_wait(bar, 8)
+
+    WB = hq // 3
+    zr, ob, lr = z * 2 * WB, WB, (1 - z) * 2 * WB
+
+    def worows(d, off=0, n=WB):
+        return woland.at[pl.ds(pl.multiple_of(d * hq + off, WB), n), :]
 
     def wo_copy(i):
         k = dict(ss=wos.at[i], rs=wor.at[i])
-        if i < 3:
-            return rcopy(wo_ref, worows(me), to=(X, Y, PT)[i], **k)
-        d, off, n, to = ((X, 0, W2, Y), (Y, W2, W2, X), (X, 0, hq, PT), (Y, 0, hq, PT), (DG, 0, W2, PT),
-                         (DG, W2, W2, PT))[i - 3]
-        return rcopy(worows(d, off, n), worows(d, off, n), to=to, **k)
+        if i < 4:
+            off = (zr, ob)[i // 2]
+            return rcopy(wo_ref.at[pl.ds(pl.multiple_of(off, WB), WB), :], worows(me, off), to=(X, Y)[i % 2], **k)
+        if i == 4:
+            return rcopy(wo_ref, worows(me, 0, hq), to=PT, **k)
+        d, off, to = ((X, zr, Y), (Y, ob, X), (X, zr, None), (Y, zr, None), (DG, zr, None), (X, zr, PT), (Y, zr, PT),
+                      (X, ob, PT), (Y, ob, PT), (DG, zr, PT), (DG, ob, PT), (X, lr, PT), (Y, lr, PT),
+                      (DG, lr, PT))[i - 5]
+        return rcopy(worows(d, off), worows(d, off), to=to, **k)
 
     def wo_recv(i):
-        d = worows(*((X,), (Y,), (PT,), (DG, 0, W2), (DG, W2, W2), (dev(cx, 1 - s),), (dev(cy, 1 - s),),
-                     (dev(cd, 1 - s), 0, W2), (dev(cd, 1 - s), W2, W2))[i])
+        x1, y1, d1 = dev(cx, 1 - s), dev(cy, 1 - s), dev(cd, 1 - s)
+        d = worows(*((X, zr), (Y, zr), (X, ob), (Y, ob), (PT, 0, hq), (DG, zr), (DG, ob), (X, lr), (Y, lr), (DG, lr),
+                     (x1, zr), (y1, zr), (x1, ob), (y1, ob), (d1, zr), (d1, ob), (x1, lr), (y1, lr), (d1, lr))[i])
         rcopy(d, d, wos.at[i], wor.at[i], PT).wait_recv()
 
+    def wo_step(recvs, sends):
+        for n in recvs:
+            wo_recv(n)
+        for n in sends:
+            wo_copy(n).start()
+
     wo_in = pltpu.make_async_copy(wo_ref, hk.at[pl.ds(0, hq), :], lsem.at[0, 0])
-    wo_out = pltpu.make_async_copy(hk.at[pl.ds(0, hq), :], worows(me), lsem.at[0, 0])
+    wo_out = pltpu.make_async_copy(hk.at[pl.ds(0, hq), :], worows(me, 0, hq), lsem.at[0, 0])
 
     def peer(m):
         return (me + m) % 8
@@ -125,8 +156,7 @@
 
             for cp in tile(0, 0) + cps:
                 cp.start()
-            for i in range(3):
-                wo_copy(i).start()
+            wo_step((), range(5))
             wo_in.start()
 
             @pl.loop(0, nb)
@@ -166,6 +196,10 @@
                 v[row, :] = zv.astype(BF)
                 vt[:, row] = zv.T.astype(BF)
 
+                @pl.when(i == nb // 2)
+                def _():
+                    wo_step((0, 1), (7, 8, 5, 10, 11))
+
         pl.run_scoped(run, pltpu.VMEM((D, hq + 2 * HEAD), BF), pltpu.VMEM((2, TM, D), BF),
                       pltpu.VMEM((2, TM, HEAD), F32), pltpu.VMEM((2, TM, HEAD), F32),
                       pltpu.SemaphoreType.DMA((2, 3)), pltpu.SemaphoreType.DMA((3,)))
@@ -177,6 +211,7 @@
             cp.start()
         wo_in.wait()
         wo_out.start()
+        wo_step((2, 3), (6, 12, 13))
         sc = (HEAD ** -0.5) * LOG2E
         nq = T // QB
         ki = lax.broadcasted_iota(jnp.int32, (QB, QB), 0)
@@ -229,26 +264,26 @@
             for h in range(nh):
                 q[row, h * HEAD:(h + 1) * HEAD] = (acc[h] / ll[h]).T.astype(BF)
 
-            per = C // QB
-
-            @pl.when(i % per == per - 1)
-            def _():
-                j = i // per
+            def send_o(j):
                 for m in range(1, 8):
                     a2a(j, m, q).start()
                 a2a_own(j, q).start()
 
-            @pl.when(i == nq // 2)
-            def _():
-                for n in (0, 1):
-                    wo_recv(n)
-                    wo_copy(n + 3).start()
-                for n in (5, 6):
-                    wo_copy(n).start()
-
-        for n in (3, 4):
-            wo_recv(n)
-            wo_copy(n + 4).start()
+            if C < QB:
+                for jj in range(QB // C):
+                    send_o(i * (QB // C) + jj)
+            else:
+                per = C // QB
+
+                @pl.when(i % per == per - 1)
+                def _():
+                    send_o(i // per)
+
+            @pl.when(i == nq * 3 // 4 - 1)
+            def _():
+                wo_step((5, 7, 8), (9, 14, 16, 17))
+
+        wo_step((6, 9), (15, 18))
         for cp in kv_out:
             cp.wait()
 
@@ -263,9 +298,8 @@
                   pltpu.VMEM((nh, 1, QB), F32), pltpu.VMEM((nh, 1, QB), F32), pltpu.VMEM((nh, 1, QB), F32),
                   pltpu.VMEM((nh, QB, QB), F32), pltpu.SemaphoreType.DMA((2,)))
     wo_out.wait()
-    for n in (2, 5, 6, 7, 8):
-        wo_recv(n)
-    for n in range(9):
+    wo_step((4,) + tuple(range(10, 19)), ())
+    for n in range(19):
         wo_copy(n).wait_send()
 
     R2 = R // 2
@@ -578,16 +612,19 @@
                             pltpu.VMEM((J, R, d // 2), BF), pltpu.VMEM((J, R, d // 2), BF),
                             pltpu.VMEM((J * R, d), BF), pltpu.VMEM((J * R, d), BF),
                             dma((J, 8)), dma((J, 8)), dma((J, 9)), dma((J, 9)), dma((J, 9)), dma((J, 9)),
-                            dma((J, 7)), dma((J, 7)), dma((9,)), dma((9,)), dma((2, J)), dma((3,))],
+                            dma((J, 7)), dma((J, 7)), dma((19,)), dma((19,)), dma((2, J)), dma((3,))],
             compiler_params=pltpu.CompilerParams(collective_id=0, has_side_effects=True,
                                                  vmem_limit_bytes=67043328),
             cost_estimate=pl.CostEstimate(flops=2 * t * d * ff * 4, bytes_accessed=2 * t * d * 6, transcendentals=0),
             name="layer",
         )(x, g1.reshape(1, d), g2.reshape(1, d), cs, sn, wq, wk, wv, wo, wg, wu, wd)
-        cb = pl.BlockSpec((min(256, t), d), lambda i: (i, 0))
-        y = pl.pallas_call(_copy_kernel, grid=(t // min(256, t),), in_specs=[cb], out_specs=cb, out_shape=big(t, d),
-                           compiler_params=pltpu.CompilerParams(dimension_semantics=("arbitrary",)),
-                           name="out")(y)
+        nt = 16
+        y, k, v = pl.pallas_call(
+            functools.partial(_copy_kernel, nt), in_specs=[ANY] * 3, out_specs=[ANY] * 3,
+            out_shape=[big(t, d), big(t, HEAD), big(t, HEAD)],
+            scratch_shapes=[pltpu.VMEM((t, d), BF), pltpu.VMEM((t, HEAD), BF), pltpu.VMEM((t, HEAD), BF),
+                            dma((nt + 2,)), dma((nt + 2,))],
+            compiler_params=pltpu.CompilerParams(vmem_limit_bytes=32 << 20), name="out")(y, k, v)
         return y, k.reshape(t, 1, HEAD), v.reshape(t, 1, HEAD)
 
     return jax.shard_map(

time: 497 us -> 483 us (0.972)
  Pallas kernels: 484 us -> 471 us
    pallas_call x1, Pallas kernels: 462 us -> 453 us  [local(): pl.pallas_call(functools.partial(_big_kernel, J, R, QB), in_specs=[ANY, v...]
where the time goes in v5:
time: 483 us
  Pallas kernels  471 us (98%)
  other arithmetic  6.36 us (1%)
  local copies, waits for them, and re-layouts  5.05 us (1%)
    pallas_call x1, Pallas kernels, local(): pl.pallas_call(functools.partial(_big_kernel, J, R, QB), in_specs=[ANY, v...  453 us
    pallas_call x1, Pallas kernels, local(): pl.pallas_call(functools.partial(_copy_kernel, nt), in_specs=[ANY] * 3, o...  17.9 us

profile of v5, /device:TPU:0, one launch (start us, length us, event | category | flops | bytes accessed | tf_op | source)
XLA Modules:
  0.0 482.6 jit_solution(2076827986654307725)
XLA Ops:
  0.7 0.1 pad_maximum_fusion
  0.7 1.3 reshape.21.g1_ref
  2.0 1.3 reshape.22.g2_ref
  3.3 0.7 convert_element_type.3
  4.1 5.5 %fusion = (f32[2048,128]{1,0:T(8,128)}, f32[2048,128]{1,0:T(8,128)}) fusion(f32[128]{0:T(128)S(1)} %pad_maximum_fusion, f32[2048]{0:T(1024)S(1)} %get-tuple-element.18, f32[2048]{0:T(1024)S(1)} %get-tuple-element.17, pred[128]{0:T(512)(128)(4,1)S(1)} %iota_compare_fusion), kind=kLoop, calls=%fused_computation.1 | loop fusion | flops 524288 | bytes 2114176 | tf_op jit(solution)/shard_map/sin | solution.py:589
  9.6 452.6 %layer.1 = (bf16[4096,3072]{1,0:T(8,128)(2,1)}, bf16[4096,128]{1,0:T(8,128)(2,1)}, bf16[4096,128]{1,0:T(8,128)(2,1)}, bf16[512,3072]{1,0:T(8,128)(2,1)}, bf16[40...) custom-call(bf16[4096,3072]{1,0:T(8,128)(2,1)} %x_ref.1, ...), custom_call_target="tpu_custom_call" | custom-call | flops 103079215104 | bytes 150994944 | tf_op jit(solution)/shard_map/layer/pallas_call | solution.py:604
  462.2 0.0 copy-start
  462.2 1.2 copy-done
  463.4 0.0 copy-start.1
  463.4 1.2 copy-done.1
  464.7 17.9 %out.1 = (bf16[4096,3072]{1,0:T(8,128)(2,1)}, bf16[4096,128]{1,0:T(8,128)(2,1)}, bf16[4096,128]{1,0:T(8,128)(2,1)}) custom-call(bf16[4096,3072]{1,0:T(8,128)(2,1)} %get-tuple-element.9.y, bf16[4096,128]{1,0:T(8,128)(2,1)S(1)} %copy-done, bf16[4096,128]{1,0:T(8,128)(2,1)S(1)} %copy-done.1), custom_call_target="tpu_custom_call" | custom-call | tf_op jit(solution)/shard_map/out/pallas_call | solution.py:622
  (3 shorter events, 0.0 us)
Async XLA Ops:
  462.2 1.2 copy-start
  463.4 1.2 copy-start.1

commit v6 on v5

--- a/solution.py
+++ b/solution.py
@@ -51,7 +51,7 @@
 
 def _big_kernel(J, R, QB, x_ref, g1_ref, g2_ref, cos_ref, sin_ref, wq_ref, wk_ref, wv_ref, wo_ref, wg_ref, wu_ref,
                 wd_ref, y_ref, kout, vout, oland, bland, rs1land, woland,
-                wg, wu, wd, rs2x, rs2y, rs3a, rs3b, hk, own,
+                wg, wu, wd, rs2x, rs2y, rs3a, rs3b, hk, own, q,
                 a2s, a2r, abs_, abr, ays, ayr, rss, rsr, wos, wor, lsem, wsem):
     me = lax.axis_index("tp")
     c, s = me // 2, me % 2
@@ -124,22 +124,31 @@
     def frm(m):
         return (me + 8 - m) % 8
 
-    def a2a(j, m, o):
+    JH = J // 2
+
+    def a2a(b, m):
         to = peer(m)
-        return rcopy(o.at[pl.ds(pl.multiple_of(j * C + _pos_of(to) * R, R), R), :],
-                     oland.at[pl.ds(pl.multiple_of(j * R, R), R), pl.ds(pl.multiple_of(me * hq, HEAD), hq)],
-                     a2s.at[j, m], a2r.at[j, m], to)
-
-    def a2a_land(j, m):
-        return oland.at[pl.ds(pl.multiple_of(j * R, R), R), pl.ds(pl.multiple_of(frm(m) * hq, HEAD), hq)]
-
-    def a2a_own(j, o):
-        return pltpu.make_async_copy(o.at[pl.ds(pl.multiple_of(j * C + mypos * R, R), R), :], a2a_land(j, 0),
-                                     a2s.at[j, 0])
+        return rcopy(q.at[pl.ds(b * JH, JH), _pos_of(to)],
+                     oland.at[pl.ds(b * JH, JH), :, pl.ds(pl.multiple_of(me * hq, HEAD), hq)],
+                     a2s.at[b, m], a2r.at[b, m], to)
+
+    def a2a_land(b, m):
+        return oland.at[pl.ds(b * JH, JH), :, pl.ds(pl.multiple_of(frm(m) * hq, HEAD), hq)]
+
+    def a2a_own(b):
+        return pltpu.make_async_copy(q.at[pl.ds(b * JH, JH), mypos], a2a_land(b, 0), a2s.at[b, 0])
+
+    def send_o(b):
+        for m in range(1, 8):
+            a2a(b, m).start()
+        a2a_own(b).start()
+
+    def qblock(i, h, n):
+        return (pl.ds(i * (n // C), n // C), slice(None), slice(None), pl.ds(h * HEAD, HEAD))
 
     TM = min(512, T // 2)
 
-    def qkv(q, k, v, vt):
+    def qkv(k, v, vt):
         def run(w, xt, ct, st, tsem, msem):
             nb = T // TM
             col = pl.ds(pl.multiple_of(me * HEAD, HEAD), HEAD)
@@ -189,7 +198,7 @@
                     t = z[:, h * HEAD:(h + 1) * HEAD]
                     t = (t * cc + pltpu.roll(t, HEAD // 2, 1) * ss).astype(BF)
                     if h < nh:
-                        q[row, h * HEAD:(h + 1) * HEAD] = t
+                        q[qblock(i, h, TM)] = t.reshape(TM // C, 8, R, HEAD)
                     else:
                         k[row, :] = t
                 zv = z[:, hq + HEAD:]
@@ -204,8 +213,8 @@
                       pltpu.VMEM((2, TM, HEAD), F32), pltpu.VMEM((2, TM, HEAD), F32),
                       pltpu.SemaphoreType.DMA((2, 3)), pltpu.SemaphoreType.DMA((3,)))
 
-    def attention(q, k, v, vt, acc, mm, ll, mx, sb, asem):
-        qkv(q, k, v, vt)
+    def attention(k, v, vt, acc, mm, ll, mx, sb, asem):
+        qkv(k, v, vt)
         kv_out = [pltpu.make_async_copy(k, kout, asem.at[0]), pltpu.make_async_copy(v, vout, asem.at[1])]
         for cp in kv_out + wcp:
             cp.start()
@@ -219,11 +228,9 @@
 
         @pl.loop(0, nq)
         def _(i):
-            row = pl.ds(pl.multiple_of(i * QB, QB), QB)
-
             def qk(kb, h, masked=False):
                 kk = k[pl.ds(pl.multiple_of(kb * QB, QB), QB), :]
-                t = lax.dot_general(kk, q[row, h * HEAD:(h + 1) * HEAD], (((1,), (1,)), ((), ())),
+                t = lax.dot_general(kk, q[qblock(i, h, QB)].reshape(QB, HEAD), (((1,), (1,)), ((), ())),
                                     preferred_element_type=F32)
                 if masked:
                     t = jnp.where(ki <= qi, t, -jnp.inf)
@@ -262,38 +269,22 @@
                 phases(kb, kb + 1, False)
 
             for h in range(nh):
-                q[row, h * HEAD:(h + 1) * HEAD] = (acc[h] / ll[h]).T.astype(BF)
-
-            def send_o(j):
-                for m in range(1, 8):
-                    a2a(j, m, q).start()
-                a2a_own(j, q).start()
-
-            if C < QB:
-                for jj in range(QB // C):
-                    send_o(i * (QB // C) + jj)
-            else:
-                per = C // QB
-
-                @pl.when(i % per == per - 1)
-                def _():
-                    send_o(i // per)
+                q[qblock(i, h, QB)] = (acc[h] / ll[h]).T.astype(BF).reshape(QB // C, 8, R, HEAD)
+
+            @pl.when(i == nq // 2 - 1)
+            def _():
+                send_o(0)
 
             @pl.when(i == nq * 3 // 4 - 1)
             def _():
                 wo_step((5, 7, 8), (9, 14, 16, 17))
 
+        send_o(1)
         wo_step((6, 9), (15, 18))
         for cp in kv_out:
             cp.wait()
 
-        @pl.loop(0, J)
-        def _(j):
-            a2a_own(j, q).wait()
-            for m in range(1, 8):
-                a2a(j, m, q).wait_send()
-
-    pl.run_scoped(attention, pltpu.VMEM((T, hq), BF), pltpu.VMEM((T, HEAD), BF), pltpu.VMEM((T, HEAD), BF),
+    pl.run_scoped(attention, pltpu.VMEM((T, HEAD), BF), pltpu.VMEM((T, HEAD), BF),
                   pltpu.VMEM((HEAD, T), BF), pltpu.VMEM((nh, HEAD, QB), F32),
                   pltpu.VMEM((nh, 1, QB), F32), pltpu.VMEM((nh, 1, QB), F32), pltpu.VMEM((nh, 1, QB), F32),
                   pltpu.VMEM((nh, QB, QB), F32), pltpu.SemaphoreType.DMA((2,)))
@@ -367,7 +358,6 @@
 
     def mlp(bt, us, pb, rt, sums, oo, wt, bsem, osem, tsem):
         NT = wt.shape[2]
-        JH = J // 2
         RH = JH * R
 
         def x_in(j):
@@ -383,13 +373,11 @@
 
             tile(0, 0).start()
 
-            @pl.loop(half * JH, (half + 1) * JH)
-            def _(j):
-                for m in range(1, 8):
-                    d = a2a_land(j, m)
-                    rcopy(d, d, a2s.at[j, m], a2r.at[j, m], PT).wait_recv()
-
-            cp = pltpu.make_async_copy(oland.at[part, :], oo, osem.at[0])
+            for m in range(1, 8):
+                d = a2a_land(half, m)
+                rcopy(d, d, a2s.at[half, m], a2r.at[half, m], PT).wait_recv()
+            a2a_own(half).wait()
+            cp = pltpu.make_async_copy(oland.at[pl.ds(half * JH, JH)], oo, osem.at[0])
             cp.start()
             cp.wait()
             for j in range(half * JH, (half + 1) * JH):
@@ -407,7 +395,7 @@
                 tile(n, slot).wait()
                 col = pl.ds(pl.multiple_of(n * NT, NT), NT)
                 hk[part, col] = (hk[part, col].astype(F32)
-                                 + jnp.dot(oo[...], wt[slot], preferred_element_type=F32)).astype(BF)
+                                 + jnp.dot(oo[...].reshape(RH, 8 * hq), wt[slot], preferred_element_type=F32)).astype(BF)
 
             _norm_rows(hk.at[part, :], g2_ref, own.at[part, :], RH)
 
@@ -558,13 +546,16 @@
             def _():
                 rs3(t - 1)
 
+        for b in range(2):
+            for m in range(1, 8):
+                a2a(b, m).wait_send()
         rs_copy(J - 1, 0).wait_send()
         for j in range(max(J - 2, 0), J):
             for i in range(1, 7):
                 rs_copy(j, i).wait_send()
 
     pl.run_scoped(mlp, pltpu.VMEM((2, R4, D), BF), pltpu.VMEM((R4, wg.shape[1]), BF), pltpu.VMEM((2, R4, D), BF),
-                  pltpu.VMEM((R4, D), BF), pltpu.VMEM((2, R4, D), BF), pltpu.VMEM((J * R // 2, 8 * hq), BF),
+                  pltpu.VMEM((R4, D), BF), pltpu.VMEM((2, R4, D), BF), pltpu.VMEM((J // 2, R, 8 * hq), BF),
                   pltpu.VMEM((2, 8 * hq, min(512, D)), BF), pltpu.SemaphoreType.DMA((3,)),
                   pltpu.SemaphoreType.DMA((1 + J,)), pltpu.SemaphoreType.DMA((2,)))
 
@@ -605,13 +596,13 @@
             functools.partial(_big_kernel, J, R, QB),
             in_specs=[ANY, vm, vm] + [ANY] * 9,
             out_specs=[ANY] * 7,
-            out_shape=[big(t, d), big(t, HEAD), big(t, HEAD), big(J * R, 8 * hq), big(t, d), big(J, 4 * R, d),
+            out_shape=[big(t, d), big(t, HEAD), big(t, HEAD), big(J, R, 8 * hq), big(t, d), big(J, 4 * R, d),
                        big(8 * hq, d)],
             scratch_shapes=[pltpu.VMEM((d, ff), BF), pltpu.VMEM((d, ff), BF), pltpu.VMEM((ff, d), BF),
                             pltpu.VMEM((J, 2, R, d // 2), BF), pltpu.VMEM((J, 2, R, d // 2), BF),
                             pltpu.VMEM((J, R, d // 2), BF), pltpu.VMEM((J, R, d // 2), BF),
-                            pltpu.VMEM((J * R, d), BF), pltpu.VMEM((J * R, d), BF),
-                            dma((J, 8)), dma((J, 8)), dma((J, 9)), dma((J, 9)), dma((J, 9)), dma((J, 9)),
+                            pltpu.VMEM((J * R, d), BF), pltpu.VMEM((J * R, d), BF), pltpu.VMEM((J, 8, R, hq), BF),
+                            dma((2, 8)), dma((2, 8)), dma((J, 9)), dma((J, 9)), dma((J, 9)), dma((J, 9)),
                             dma((J, 7)), dma((J, 7)), dma((19,)), dma((19,)), dma((2, J)), dma((3,))],
             compiler_params=pltpu.CompilerParams(collective_id=0, has_side_effects=True,
                                                  vmem_limit_bytes=67043328),

time: 483 us -> 476 us (0.986)
  Pallas kernels: 471 us -> 464 us
    pallas_call x1, Pallas kernels: 453 us -> 446 us  [local(): pl.pallas_call(functools.partial(_big_kernel, J, R, QB), in_specs=[ANY, v...]
where the time goes in v6:
time: 476 us
  Pallas kernels  464 us (97%)
  other arithmetic  6.36 us (1%)
  local copies, waits for them, and re-layouts  5.05 us (1%)
    pallas_call x1, Pallas kernels, local(): pl.pallas_call(functools.partial(_big_kernel, J, R, QB), in_specs=[ANY, v...  446 us
    pallas_call x1, Pallas kernels, local(): pl.pallas_call(functools.partial(_copy_kernel, nt), in_specs=[ANY] * 3, o...  17.9 us

profile of v6, /device:TPU:0, one launch (start us, length us, event | category | flops | bytes accessed | tf_op | source)
XLA Modules:
  0.0 475.6 jit_solution(14659046229515444252)
XLA Ops:
  0.7 0.1 pad_maximum_fusion
  0.7 1.3 reshape.21.g1_ref
  2.0 1.3 reshape.22.g2_ref
  3.3 0.7 convert_element_type.3
  4.1 5.5 %fusion = (f32[2048,128]{1,0:T(8,128)}, f32[2048,128]{1,0:T(8,128)}) fusion(f32[128]{0:T(128)S(1)} %pad_maximum_fusion, f32[2048]{0:T(1024)S(1)} %get-tuple-element.18, f32[2048]{0:T(1024)S(1)} %get-tuple-element.17, pred[128]{0:T(512)(128)(4,1)S(1)} %iota_compare_fusion), kind=kLoop, calls=%fused_computation.1 | loop fusion | flops 524288 | bytes 2114176 | tf_op jit(solution)/shard_map/sin | solution.py:580
  9.6 445.6 %layer.1 = (bf16[4096,3072]{1,0:T(8,128)(2,1)}, bf16[4096,128]{1,0:T(8,128)(2,1)}, bf16[4096,128]{1,0:T(8,128)(2,1)}, bf16[8,64,3072]{2,1,0:T(8,128)(2,1)}, bf16...) custom-call(bf16[4096,3072]{1,0:T(8,128)(2,1)} %x_ref.1, ...), custom_call_target="tpu_custom_call" | custom-call | flops 103079215104 | bytes 150994944 | tf_op jit(solution)/shard_map/layer/pallas_call | solution.py:595
  455.2 0.0 copy-start
  455.3 1.2 copy-done
  456.5 0.0 copy-start.1
  456.5 1.2 copy-done.1
  457.7 17.9 %out.1 = (bf16[4096,3072]{1,0:T(8,128)(2,1)}, bf16[4096,128]{1,0:T(8,128)(2,1)}, bf16[4096,128]{1,0:T(8,128)(2,1)}) custom-call(bf16[4096,3072]{1,0:T(8,128)(2,1)} %get-tuple-element.9.y, bf16[4096,128]{1,0:T(8,128)(2,1)S(1)} %copy-done, bf16[4096,128]{1,0:T(8,128)(2,1)S(1)} %copy-done.1), custom_call_target="tpu_custom_call" | custom-call | tf_op jit(solution)/shard_map/out/pallas_call | solution.py:613
  (3 shorter events, 0.0 us)
Async XLA Ops:
  455.2 1.2 copy-start
  456.5 1.2 copy-start.1

commit v7 on v6

--- a/solution.py
+++ b/solution.py
@@ -27,7 +27,7 @@
         sl = pl.ds(pl.multiple_of(n * step, step), step)
         t = src[sl, :].astype(F32)
         inv = lax.rsqrt(jnp.mean(t * t, axis=-1, keepdims=True) + EPS)
-        dst[sl, :] = (t * inv * g_ref[...].astype(F32)).astype(BF)
+        dst[sl, :] = (t * inv * g_ref[...]).astype(BF)
 
 
 def _copy_kernel(nt, y, k, v, yo, ko, vo, yb, kb, vb, si, so):
@@ -49,7 +49,7 @@
         cp.wait()
 
 
-def _big_kernel(J, R, QB, x_ref, g1_ref, g2_ref, cos_ref, sin_ref, wq_ref, wk_ref, wv_ref, wo_ref, wg_ref, wu_ref,
+def _big_kernel(J, R, QB, x_ref, g_ref, cos_ref, sin_ref, wq_ref, wk_ref, wv_ref, wo_ref, wg_ref, wu_ref,
                 wd_ref, y_ref, kout, vout, oland, bland, rs1land, woland,
                 wg, wu, wd, rs2x, rs2y, rs3a, rs3b, hk, own, q,
                 a2s, a2r, abs_, abr, ays, ayr, rss, rsr, wos, wor, lsem, wsem):
@@ -57,6 +57,7 @@
     c, s = me // 2, me % 2
     T, D = x_ref.shape
     H = D // 2
+    g1_ref, g2_ref = g_ref.at[pl.ds(0, 1), :], g_ref.at[pl.ds(1, 1), :]
     C = 8 * R
     R4 = 4 * R
     hq = wq_ref.shape[1]
@@ -129,11 +130,11 @@
     def a2a(b, m):
         to = peer(m)
         return rcopy(q.at[pl.ds(b * JH, JH), _pos_of(to)],
-                     oland.at[pl.ds(b * JH, JH), :, pl.ds(pl.multiple_of(me * hq, HEAD), hq)],
+                     oland.at[me, pl.ds(b * JH, JH)],
                      a2s.at[b, m], a2r.at[b, m], to)
 
     def a2a_land(b, m):
-        return oland.at[pl.ds(b * JH, JH), :, pl.ds(pl.multiple_of(frm(m) * hq, HEAD), hq)]
+        return oland.at[frm(m), pl.ds(b * JH, JH)]
 
     def a2a_own(b):
         return pltpu.make_async_copy(q.at[pl.ds(b * JH, JH), mypos], a2a_land(b, 0), a2s.at[b, 0])
@@ -279,7 +280,6 @@
             def _():
                 wo_step((5, 7, 8), (9, 14, 16, 17))
 
-        send_o(1)
         wo_step((6, 9), (15, 18))
         for cp in kv_out:
             cp.wait()
@@ -362,7 +362,7 @@
 
         def x_in(j):
             return pltpu.make_async_copy(x_ref.at[pl.ds(pl.multiple_of(j * C + mypos * R, R), R), :],
-                                         hk.at[pl.ds(pl.multiple_of(j * R, R), R), :], osem.at[1 + j])
+                                         hk.at[pl.ds(pl.multiple_of(j * R, R), R), :], osem.at[j])
 
         def oproj(half):
             part = pl.ds(half * RH, RH)
@@ -377,9 +377,12 @@
                 d = a2a_land(half, m)
                 rcopy(d, d, a2s.at[half, m], a2r.at[half, m], PT).wait_recv()
             a2a_own(half).wait()
-            cp = pltpu.make_async_copy(oland.at[pl.ds(half * JH, JH)], oo, osem.at[0])
-            cp.start()
-            cp.wait()
+            cps = [pltpu.make_async_copy(oland.at[d, pl.ds(half * JH, JH)], oo.at[:, :, pl.ds(d * hq, hq)],
+                                         osem.at[J + d]) for d in range(8)]
+            for cp in cps:
+                cp.start()
+            for cp in cps:
+                cp.wait()
             for j in range(half * JH, (half + 1) * JH):
                 x_in(j).wait()
             nt = D // NT
@@ -501,9 +504,9 @@
         g_own(*gb, 0, 0)
         for cp in wcp:
             cp.wait()
-        oproj(1)
         g_fwd(*gb, 0)
         g_own(*gb, 1, 0)
+        send_o(1)
 
         @pl.loop(0, J + 4)
         def _(t):
@@ -545,6 +548,10 @@
             @pl.when(jnp.logical_and(t >= 1, t < J + 1))
             def _():
                 rs3(t - 1)
+
+            @pl.when(t == 0)
+            def _():
+                oproj(1)
 
         for b in range(2):
             for m in range(1, 8):
@@ -557,7 +564,7 @@
     pl.run_scoped(mlp, pltpu.VMEM((2, R4, D), BF), pltpu.VMEM((R4, wg.shape[1]), BF), pltpu.VMEM((2, R4, D), BF),
                   pltpu.VMEM((R4, D), BF), pltpu.VMEM((2, R4, D), BF), pltpu.VMEM((J // 2, R, 8 * hq), BF),
                   pltpu.VMEM((2, 8 * hq, min(512, D)), BF), pltpu.SemaphoreType.DMA((3,)),
-                  pltpu.SemaphoreType.DMA((1 + J,)), pltpu.SemaphoreType.DMA((2,)))
+                  pltpu.SemaphoreType.DMA((8 + J,)), pltpu.SemaphoreType.DMA((2,)))
 
     @pl.loop(0, J)
     def _(j):
@@ -594,9 +601,9 @@
         big = lambda *sh: jax.ShapeDtypeStruct(sh, BF)
         y, k, v, *_ = pl.pallas_call(
             functools.partial(_big_kernel, J, R, QB),
-            in_specs=[ANY, vm, vm] + [ANY] * 9,
+            in_specs=[ANY, vm] + [ANY] * 9,
             out_specs=[ANY] * 7,
-            out_shape=[big(t, d), big(t, HEAD), big(t, HEAD), big(J, R, 8 * hq), big(t, d), big(J, 4 * R, d),
+            out_shape=[big(t, d), big(t, HEAD), big(t, HEAD), big(8, J, R, hq), big(t, d), big(J, 4 * R, d),
                        big(8 * hq, d)],
             scratch_shapes=[pltpu.VMEM((d, ff), BF), pltpu.VMEM((d, ff), BF), pltpu.VMEM((ff, d), BF),
                             pltpu.VMEM((J, 2, R, d // 2), BF), pltpu.VMEM((J, 2, R, d // 2), BF),
@@ -608,14 +615,14 @@
                                                  vmem_limit_bytes=67043328),
             cost_estimate=pl.CostEstimate(flops=2 * t * d * ff * 4, bytes_accessed=2 * t * d * 6, transcendentals=0),
             name="layer",
-        )(x, g1.reshape(1, d), g2.reshape(1, d), cs, sn, wq, wk, wv, wo, wg, wu, wd)
+        )(x, jnp.stack([g1, g2]).astype(F32), cs, sn, wq, wk, wv, wo, wg, wu, wd)
         nt = 16
         y, k, v = pl.pallas_call(
             functools.partial(_copy_kernel, nt), in_specs=[ANY] * 3, out_specs=[ANY] * 3,
             out_shape=[big(t, d), big(t, HEAD), big(t, HEAD)],
             scratch_shapes=[pltpu.VMEM((t, d), BF), pltpu.VMEM((t, HEAD), BF), pltpu.VMEM((t, HEAD), BF),
                             dma((nt + 2,)), dma((nt + 2,))],
-            compiler_params=pltpu.CompilerParams(vmem_limit_bytes=32 << 20), name="out")(y, k, v)
+            compiler_params=pltpu.CompilerParams(vmem_limit_bytes=67043328), name="out")(y, k, v)
         return y, k.reshape(t, 1, HEAD), v.reshape(t, 1, HEAD)
 
     return jax.shard_map(

time: 476 us -> 489 us (1.027)
  Pallas kernels: 464 us -> 479 us
    pallas_call x1, Pallas kernels: 446 us -> 460 us  [local(): pl.pallas_call(functools.partial(_big_kernel, J, R, QB), in_specs=[ANY, v...]
where the time goes in v7:
time: 489 us; the launch traced here: 488 us
  Pallas kernels  479 us (98%)
  other arithmetic  7 us (1%)
    pallas_call x1, Pallas kernels, local(): pl.pallas_call(functools.partial(_big_kernel, J, R, QB), in_specs=[ANY, v...  460 us
    pallas_call x1, Pallas kernels, local(): pl.pallas_call(functools.partial(_copy_kernel, nt), in_specs=[ANY] * 3, o...  18.5 us

profile of v7, /device:TPU:0, one launch (start us, length us, event | category | flops | bytes accessed | tf_op | source)
XLA Modules:
  0.0 488.0 jit_solution(12969759736807424671)
XLA Ops:
  0.7 0.1 pad_maximum_fusion
  0.7 0.7 stack.9
  1.4 0.7 stack.10
  2.1 0.6 maximum_convert_fusion.g_ref
  2.8 0.7 convert_element_type.7
  3.5 5.5 %fusion = (f32[2048,128]{1,0:T(8,128)}, f32[2048,128]{1,0:T(8,128)}) fusion(f32[128]{0:T(128)S(1)} %pad_maximum_fusion, f32[2048]{0:T(1024)S(1)} %get-tuple-element.18, f32[2048]{0:T(1024)S(1)} %get-tuple-element.17, pred[128]{0:T(512)(128)(4,1)S(1)} %iota_compare_fusion), kind=kLoop, calls=%fused_computation.1 | loop fusion | flops 524288 | bytes 2114176 | tf_op jit(solution)/shard_map/sin | solution.py:587
  9.1 460.4 %layer.1 = (bf16[4096,3072]{1,0:T(8,128)(2,1)}, bf16[4096,128]{1,0:T(8,128)(2,1)}, bf16[4096,128]{1,0:T(8,128)(2,1)}, bf16[8,8,64,384]{3,2,1,0:T(8,128)(2,1)}, b...) custom-call(bf16[4096,3072]{1,0:T(8,128)(2,1)} %x_ref.1, ...), custom_call_target="tpu_custom_call" | custom-call | flops 103079215104 | bytes 150994944 | tf_op jit(solution)/shard_map/layer/pallas_call | solution.py:602
  469.5 18.5 %out.1 = (bf16[4096,3072]{1,0:T(8,128)(2,1)}, bf16[4096,128]{1,0:T(8,128)(2,1)}, bf16[4096,128]{1,0:T(8,128)(2,1)}) custom-call(bf16[4096,3072]{1,0:T(8,128)(2,1)} %get-tuple-element.9.y, bf16[4096,128]{1,0:T(8,128)(2,1)} %get-tuple-element.10.k, bf16[4096,128]{1,0:T(8,128)(2,1)} %get-tuple-element.11.v), custom_call_target="tpu_custom_call" | custom-call | tf_op jit(solution)/shard_map/out/pallas_call | solution.py:620
  (3 shorter events, 0.0 us)

commit v8 on v7

--- a/solution.py
+++ b/solution.py
@@ -278,9 +278,12 @@
 
             @pl.when(i == nq * 3 // 4 - 1)
             def _():
-                wo_step((5, 7, 8), (9, 14, 16, 17))
-
-        wo_step((6, 9), (15, 18))
+                wo_step((5,), (9, 14))
+
+        send_o(1)
+        wo_step((6,), (15,))
+        wo_step((7, 8), (16, 17))
+        wo_step((9,), (18,))
         for cp in kv_out:
             cp.wait()
 
@@ -504,9 +507,9 @@
         g_own(*gb, 0, 0)
         for cp in wcp:
             cp.wait()
+        oproj(1)
         g_fwd(*gb, 0)
         g_own(*gb, 1, 0)
-        send_o(1)
 
         @pl.loop(0, J + 4)
         def _(t):
@@ -548,10 +551,6 @@
             @pl.when(jnp.logical_and(t >= 1, t < J + 1))
             def _():
                 rs3(t - 1)
-
-            @pl.when(t == 0)
-            def _():
-                oproj(1)
 
         for b in range(2):
             for m in range(1, 8):

time: 489 us -> 472 us (0.965)
  Pallas kernels: 479 us -> 462 us
    pallas_call x1, Pallas kernels: 460 us -> 443 us  [local(): pl.pallas_call(functools.partial(_big_kernel, J, R, QB), in_specs=[ANY, v...]
where the time goes in v8:
time: 472 us; the launch traced here: 471 us
  Pallas kernels  462 us (98%)
  other arithmetic  7 us (1%)
    pallas_call x1, Pallas kernels, local(): pl.pallas_call(functools.partial(_big_kernel, J, R, QB), in_specs=[ANY, v...  443 us
    pallas_call x1, Pallas kernels, local(): pl.pallas_call(functools.partial(_copy_kernel, nt), in_specs=[ANY] * 3, o...  18.5 us

profile of v8, /device:TPU:0, one launch (start us, length us, event | category | flops | bytes accessed | tf_op | source)
XLA Modules:
  0.0 471.0 jit_solution(3881717354338572352)
XLA Ops:
  0.7 0.1 pad_maximum_fusion
  0.7 0.7 stack.9
  1.4 0.7 stack.10
  2.1 0.6 maximum_convert_fusion.g_ref
  2.8 0.7 convert_element_type.7
  3.5 5.5 %fusion = (f32[2048,128]{1,0:T(8,128)}, f32[2048,128]{1,0:T(8,128)}) fusion(f32[128]{0:T(128)S(1)} %pad_maximum_fusion, f32[2048]{0:T(1024)S(1)} %get-tuple-element.18, f32[2048]{0:T(1024)S(1)} %get-tuple-element.17, pred[128]{0:T(512)(128)(4,1)S(1)} %iota_compare_fusion), kind=kLoop, calls=%fused_computation.1 | loop fusion | flops 524288 | bytes 2114176 | tf_op jit(solution)/shard_map/sin | solution.py:586
  9.1 443.4 %layer.1 = (bf16[4096,3072]{1,0:T(8,128)(2,1)}, bf16[4096,128]{1,0:T(8,128)(2,1)}, bf16[4096,128]{1,0:T(8,128)(2,1)}, bf16[8,8,64,384]{3,2,1,0:T(8,128)(2,1)}, b...) custom-call(bf16[4096,3072]{1,0:T(8,128)(2,1)} %x_ref.1, ...), custom_call_target="tpu_custom_call" | custom-call | flops 103079215104 | bytes 150994944 | tf_op jit(solution)/shard_map/layer/pallas_call | solution.py:601
  452.5 18.5 %out.1 = (bf16[4096,3072]{1,0:T(8,128)(2,1)}, bf16[4096,128]{1,0:T(8,128)(2,1)}, bf16[4096,128]{1,0:T(8,128)(2,1)}) custom-call(bf16[4096,3072]{1,0:T(8,128)(2,1)} %get-tuple-element.9.y, bf16[4096,128]{1,0:T(8,128)(2,1)} %get-tuple-element.10.k, bf16[4096,128]{1,0:T(8,128)(2,1)} %get-tuple-element.11.v), custom_call_target="tpu_custom_call" | custom-call | tf_op jit(solution)/shard_map/out/pallas_call | solution.py:619
  (3 shorter events, 0.0 us)

commit v9 on v8

--- a/solution.py
+++ b/solution.py
@@ -11,7 +11,7 @@
 EPS = 1e-5
 ROPE_BASE = 500000.0
 LOG2E = 1.4426950408889634
-NCHUNK = 8
+NCHUNK = 16
 MESH = pl.DeviceIdType.MESH
 F32, BF = jnp.float32, jnp.bfloat16
 ANY = pl.BlockSpec(memory_space=pl.ANY)

time: 472 us -> 528 us (1.12)
  Pallas kernels: 462 us -> 517 us
    pallas_call x1, Pallas kernels: 443 us -> 499 us  [local(): pl.pallas_call(functools.partial(_big_kernel, J, R, QB), in_specs=[ANY, v...]
where the time goes in v9:
time: 528 us; the launch traced here: 526 us
  Pallas kernels  517 us (98%)
  other arithmetic  7 us (1%)
    pallas_call x1, Pallas kernels, local(): pl.pallas_call(functools.partial(_big_kernel, J, R, QB), in_specs=[ANY, v...  499 us
    pallas_call x1, Pallas kernels, local(): pl.pallas_call(functools.partial(_copy_kernel, nt), in_specs=[ANY] * 3, o...  18.5 us

profile of v9, /device:TPU:0, one launch (start us, length us, event | category | flops | bytes accessed | tf_op | source)
XLA Modules:
  0.0 526.3 jit_solution(2579099227911097158)
XLA Ops:
  0.7 0.1 pad_maximum_fusion
  0.7 0.7 stack.9
  1.4 0.7 stack.10
  2.1 0.6 maximum_convert_fusion.g_ref
  2.8 0.7 convert_element_type.7
  3.5 5.5 %fusion = (f32[2048,128]{1,0:T(8,128)}, f32[2048,128]{1,0:T(8,128)}) fusion(f32[128]{0:T(128)S(1)} %pad_maximum_fusion, f32[2048]{0:T(1024)S(1)} %get-tuple-element.18, f32[2048]{0:T(1024)S(1)} %get-tuple-element.17, pred[128]{0:T(512)(128)(4,1)S(1)} %iota_compare_fusion), kind=kLoop, calls=%fused_computation.1 | loop fusion | flops 524288 | bytes 2114176 | tf_op jit(solution)/shard_map/sin | solution.py:586
  9.1 498.7 %layer.1 = (bf16[4096,3072]{1,0:T(8,128)(2,1)}, bf16[4096,128]{1,0:T(8,128)(2,1)}, bf16[4096,128]{1,0:T(8,128)(2,1)}, bf16[8,16,32,384]{3,2,1,0:T(8,128)(2,1)}, ...) custom-call(bf16[4096,3072]{1,0:T(8,128)(2,1)} %x_ref.1, ...), custom_call_target="tpu_custom_call" | custom-call | flops 103079215104 | bytes 150994944 | tf_op jit(solution)/shard_map/layer/pallas_call | solution.py:601
  507.7 18.5 %out.1 = (bf16[4096,3072]{1,0:T(8,128)(2,1)}, bf16[4096,128]{1,0:T(8,128)(2,1)}, bf16[4096,128]{1,0:T(8,128)(2,1)}) custom-call(bf16[4096,3072]{1,0:T(8,128)(2,1)} %get-tuple-element.9.y, bf16[4096,128]{1,0:T(8,128)(2,1)} %get-tuple-element.10.k, bf16[4096,128]{1,0:T(8,128)(2,1)} %get-tuple-element.11.v), custom_call_target="tpu_custom_call" | custom-call | tf_op jit(solution)/shard_map/out/pallas_call | solution.py:619
  (3 shorter events, 0.0 us)
